TPU v7x, 32 devices: a whole 2x2x4 slice. The times are simulated.
32 devices in a mesh: ctx: 16 (over z, y, x), head: 2 (over core).
Axes of the slice: x: 2, y: 2, z: 4, core: 2. Of those that a mesh axis runs over, the one named last changes fastest.
Arguments:
- compressed: bfloat16 [3072, 576], P('ctx'), may hold values from -40 to 40
- query: bfloat16 [3072, 128, 192], P('ctx', 'head'), may hold values from -100 to 100
- d_output: bfloat16 [3072, 128, 128], P('ctx', 'head'), may hold values from -6 to 6
- w_uk: bfloat16 [512, 128, 128], P(None, 'head'), may hold values from -0.25 to 0.25
- w_uv: bfloat16 [512, 128, 128], P(None, 'head'), may hold values from -0.25 to 0.25
Outputs:
- d_query: float32 [3072, 128, 192], P('ctx', 'head')
- d_compressed: float32 [3072, 576], P(('ctx', 'head'))
- d_w_uk: float32 [512, 128, 128], P('ctx', 'head')
- d_w_uv: float32 [512, 128, 128], P('ctx', 'head')
All inputs are finite; a program needn't handle non-finite values.
Results may differ from a plain program's by a relative error of at most 0.012.
Values may be sent and summed in bfloat16 or wider, within the bound.
No kernel may reach another device: no remote copies, remote signals or barrier semaphores. Data moves between devices by JAX's collectives and lax.ppermute only.
A program may use at most 256 MiB of HBM per device.

v0:
```python
import math

import jax
import jax.numpy as jnp
from jax import lax
from jax.sharding import PartitionSpec as P

GROUP = 4


def partner(value, axis, apart):
    return lax.ppermute(value, axis, [(i, i ^ 1 << apart) for i in range(lax.axis_size(axis))])


def split_halves(stacked, upper_half):
    half_rows = stacked.shape[1] // 2
    kept_part = jnp.where(upper_half, stacked[:, half_rows:], stacked[:, :half_rows])
    outgoing = jnp.where(upper_half, stacked[:, :half_rows], stacked[:, half_rows:])
    return (kept_part, outgoing)


def per_device(compressed, query, d_output, w_uk, w_uv):
    rows_own = compressed.shape[0]
    latent_width = w_uk.shape[0]
    heads_here = w_uk.shape[1]
    nope_width = w_uk.shape[2]
    value_width = w_uv.shape[2]
    score_scale = 1.0 / math.sqrt(query.shape[2])
    levels = GROUP.bit_length() - 1
    position = lax.axis_index("ctx")
    gathered = compressed
    for bit_index in range(levels):
        partner_rows = partner(gathered, "ctx", bit_index)
        upper_half = position >> bit_index & 1 == 1
        gathered = jnp.concatenate(
            [
                jnp.where(upper_half, partner_rows, gathered),
                jnp.where(upper_half, gathered, partner_rows),
            ],
            axis=0,
        )
    span_rows = gathered.shape[0]
    latent = gathered[:, :latent_width]
    key_rope = gathered[:, latent_width:]
    weights = jnp.concatenate(
        [w_uk.reshape(latent_width, -1), w_uv.reshape(latent_width, -1)], axis=1
    )
    expanded = jnp.dot(latent, weights, preferred_element_type=jnp.float32).astype(jnp.bfloat16)
    split_at = heads_here * nope_width
    key_nope = expanded[:, :split_at].reshape(span_rows, heads_here, nope_width)
    values_here = expanded[:, split_at:].reshape(span_rows, heads_here, value_width)
    query_nope = query[..., :nope_width]
    query_rope = query[..., nope_width:]
    scores = jnp.einsum("ihd,jhd->hij", query_nope, key_nope, preferred_element_type=jnp.float32)
    scores = (
        scores + jnp.einsum("ihr,jr->hij", query_rope, key_rope, preferred_element_type=jnp.float32)
    ) * score_scale
    probs = jax.nn.softmax(scores, axis=-1)
    probs_low = probs.astype(jnp.bfloat16)
    attended = jnp.einsum(
        "hij,jhd->ihd", probs_low, values_here, preferred_element_type=jnp.float32
    )
    row_delta = jnp.sum(d_output.astype(jnp.float32) * attended, axis=-1)
    grad_probs = jnp.einsum(
        "ihd,jhd->hij", d_output, values_here, preferred_element_type=jnp.float32
    )
    score_grads = probs * (grad_probs - jnp.transpose(row_delta)[:, :, None])
    score_low = score_grads.astype(jnp.bfloat16)
    grad_nope = jnp.einsum("hij,jhd->ihd", score_low, key_nope, preferred_element_type=jnp.float32)
    grad_rope = jnp.einsum("hij,jr->ihr", score_low, key_rope, preferred_element_type=jnp.float32)
    d_query = jnp.concatenate([grad_nope, grad_rope], axis=-1) * score_scale
    key_grad = (
        jnp.einsum("hij,ihd->jhd", score_low, query_nope, preferred_element_type=jnp.float32)
        * score_scale
    ).astype(jnp.bfloat16)
    value_grad = jnp.einsum(
        "hij,ihd->jhd", probs_low, d_output, preferred_element_type=jnp.float32
    ).astype(jnp.bfloat16)
    rope_grad = (
        jnp.einsum("hij,ihr->jr", score_low, query_rope, preferred_element_type=jnp.float32)
        * score_scale
    )
    key_value = jnp.concatenate(
        [key_grad.reshape(span_rows, -1), value_grad.reshape(span_rows, -1)], axis=1
    )
    latent_grad = lax.dot_general(
        key_value, weights, (((1,), (1,)), ((), ())), preferred_element_type=jnp.float32
    )
    partial_value = jnp.concatenate([latent_grad, rope_grad], axis=1)
    column_count = partial_value.shape[1]
    stacked = partial_value.reshape(GROUP, rows_own, column_count)[None]
    for bit_index in reversed(range(levels)):
        upper_half = position >> bit_index & 1 == 1
        kept_part, outgoing = split_halves(stacked, upper_half)
        incoming = partner(outgoing, "ctx", bit_index)
        stacked = kept_part + incoming
    d_compressed = lax.psum_scatter(stacked[0, 0], "head", scatter_dimension=0, tiled=True)
    rows_each = latent_width // lax.axis_size("ctx")
    summed = lax.psum_scatter(
        lax.dot_general(
            latent, key_value, (((0,), (0,)), ((), ())), preferred_element_type=jnp.float32
        ),
        "ctx",
        scatter_dimension=0,
        tiled=True,
    )
    d_w_uk = summed[:, :split_at].reshape(rows_each, heads_here, nope_width)
    d_w_uv = summed[:, split_at:].reshape(rows_each, heads_here, value_width)
    return (d_query, d_compressed, d_w_uk, d_w_uv)


def solution(mesh):
    placed = (
        P("ctx", None),
        P("ctx", "head", None),
        P("ctx", "head", None),
        P(None, "head", None),
        P(None, "head", None),
    )
    return jax.shard_map(
        per_device,
        mesh=mesh,
        in_specs=placed,
        out_specs=(
            P("ctx", "head", None),
            P(("ctx", "head"), None),
            P("ctx", "head", None),
            P("ctx", "head", None),
        ),
        check_vma=False,
    )
```

profile of v0, /device:TPU:0, one launch (start us, length us, event | category | flops | bytes accessed | tf_op | source)
XLA Modules:
  0.0 1006.4 jit_solution(18027157554576172542)
XLA Ops:
  7.2 0.0 reduce-scatter.5.cloned.1.call-start
  7.2 1.1 copy.25
  8.3 3.0 collective-permute-start
  11.3 23.8 %bitcast_dynamic-update-slice_fusion.1 = bf16[512,16384]{1,0:T(8,128)(2,1)} fusion(bf16[64,8,64,128]{3,2,1,0:T(8,128)(2,1)} %bitcast.92), kind=kLoop, calls=%fused_computation.28 | loop fusion | bytes 16777216
  35.2 0.2 pad_maximum_fusion.4
  35.4 1.6 collective-permute-start.1
  37.0 23.9 %bitcast_dynamic-update-slice_fusion = bf16[512,16384]{1,0:T(8,128)(2,1)} fusion(bf16[512,16384]{1,0:T(8,128)(2,1)} %bitcast_dynamic-update-slice_fusion.1, bf16[64,8,64,128]{3,2,1,0:T(8,128)(2,1)} %bitcast.93), kind=kLoop, calls=%fused_computation.27 | loop fusion | bytes 16777216 | tf_op jit(solution)/shard_map/concatenate | solution.py:45
  60.8 4.2 slice.42
  65.0 4.2 slice.44
  69.3 4.2 copy.42
  73.5 1.6 broadcast_select_fusion.1
  75.2 0.0 copy-start.5
  75.2 0.7 copy-done.5
  75.9 22.8 %convolution_convert_fusion = bf16[768,16384]{1,0:T(8,128)(2,1)} fusion(bf16[512,16384]{1,0:T(8,128)(2,1)} %bitcast_dynamic-update-slice_fusion, bf16[384,576]{0,1:T(8,128)(2,1)S(1)} %get-tuple-element.16, bf16[384,576]{0,1:T(8,128)(2,1)} %copy-done.5), kind=kOutput, calls=%fused_computation.6 | convolution fusion | flops 12899057664 | bytes 42827776 | tf_op jit(solution)/shard_map/dot_general | solution.py:48
  98.8 17.4 %slice_bitcast_fusion = (bf16[96,64,8,128]{3,2,1,0:T(8,128)(2,1)}, bf16[96,64,8,128]{3,2,1,0:T(8,128)(2,1)}) fusion(bf16[768,16384]{1,0:T(8,128)(2,1)} %convolution_convert_fusion), kind=kLoop, calls=%fused_computation.20 | loop fusion | bytes 50331648
  116.2 20.3 %fusion.9 = f32[64,768,192]{1,2,0:T(8,128)} fusion(bf16[96,64,8,128]{3,2,1,0:T(8,128)(2,1)} %get-tuple-element.13, bf16[192,64,128]{2,1,0:T(8,128)(2,1)} %slice.42), kind=kOutput, calls=%fused_computation.16 | convolution fusion | flops 2415919104 | bytes 53477376 | tf_op jit(solution)/shard_map/ihd,jhd->hij/dot_general | solution.py:54
  136.5 29.1 %fusion.36 = (f32[64,192]{1,0:T(8,128)S(1)}, f32[64,192,768]{2,1,0:T(8,128)}) fusion(f32[64,768,192]{1,2,0:T(8,128)} %fusion.9, bf16[768,64,1]{0,1,2:T(8,128)(2,1)S(1)} %fusion.29, bf16[192,64,64]{0,2,1:T(8,128)(2,1)S(1)} %copy.42), kind=kOutput, calls=%fused_computation.61 | convolution fusion | flops 1245709056 | bytes 77217792 | tf_op jit(solution)/shard_map/sub | solution.py:58
  165.6 22.5 %fusion.5 = bf16[64,192,768]{2,1,0:T(8,128)(2,1)} fusion(f32[64,192,768]{2,1,0:T(8,128)} %get-tuple-element.21, f32[64,192]{1,0:T(8,128)S(1)} %get-tuple-element.20), kind=kLoop, calls=%fused_computation.12 | loop fusion | flops 18874368 | bytes 56672256 | tf_op jit(solution)/shard_map/convert_element_type | solution.py:59
  188.1 17.4 %convolution_convert_fusion.1 = bf16[64,768,128]{1,2,0:T(8,128)(2,1)} fusion(bf16[64,192,768]{2,1,0:T(8,128)(2,1)} %fusion.5, bf16[192,64,128]{2,1,0:T(8,128)(2,1)S(1)} %copy-done.3), kind=kOutput, calls=%fused_computation.29 | convolution fusion | flops 2422210560 | bytes 34603008 | tf_op jit(solution)/shard_map/hij,ihd->jhd/dot_general | solution.py:76
  205.5 15.6 %fusion.17 = f32[192,64]{0,1:T(8,128)S(1)} fusion(bf16[64,192,768]{2,1,0:T(8,128)(2,1)} %fusion.5, bf16[96,64,8,128]{3,2,1,0:T(8,128)(2,1)} %get-tuple-element.12, bf16[192,64,128]{2,1,0:T(8,128)(2,1)S(1)} %copy-done.3), kind=kOutput, calls=%fused_computation.31 | convolution fusion | flops 2420625408 | bytes 34652160 | tf_op jit(solution)/shard_map/hij,jhd->ihd/dot_general | solution.py:60
  221.1 25.5 %fusion.1 = bf16[64,192,768]{2,1,0:T(8,128)(2,1)} fusion(f32[64,192]{1,0:T(8,128)S(1)} %bitcast.98, f32[64,192,768]{2,1,0:T(8,128)} %get-tuple-element.21, f32[64,192]{1,0:T(8,128)S(1)} %get-tuple-element.20, bf16[96,64,8,128]{3,2,1,0:T(8,128)(2,1)} %get-tuple-element.12, bf16[192,64,128]{2,1,0:T(8,128)(2,1)} %param.7), kind=kOutput, calls=%fused_computation.2 | convolution fusion | flops 2453667840 | bytes 72450048 | tf_op jit(solution)/shard_map/ihd,jhd->hij/dot_general | solution.py:64
  246.6 17.4 %multiply_convert_fusion = bf16[64,768,128]{1,2,0:T(8,128)(2,1)} fusion(bf16[64,192,768]{2,1,0:T(8,128)(2,1)} %fusion.1, bf16[192,64,128]{2,1,0:T(8,128)(2,1)S(1)} %copy-done.2), kind=kOutput, calls=%fused_computation.8 | convolution fusion | flops 2428502016 | bytes 34603008 | tf_op jit(solution)/shard_map/hij,ihd->jhd/dot_general | solution.py:73
  264.0 24.8 %fusion.3 = f32[512,16384]{1,0:T(8,128)} fusion(bf16[768,8192]{0,1:T(8,128)(2,1)} %bitcast.88, bf16[768,8192]{0,1:T(8,128)(2,1)} %bitcast.96, bf16[384,576]{0,1:T(8,128)(2,1)} %copy-done.4, bf16[384,576]{0,1:T(8,128)(2,1)} %copy-done.5), kind=kOutput, calls=%fused_computation.10 | convolution fusion | flops 12936806400 | bytes 59604992 | tf_op jit(solution)/shard_map/dot_general | solution.py:100
  288.8 0.0 reduce-scatter.5.cloned.1.call-update
  288.8 0.0 reduce-scatter.3.cloned.1.call-start
  288.9 1.5 copy-done.1
  290.4 9.1 fusion.27
  299.6 22.0 %fusion.4 = f32[768,512]{0,1:T(8,128)S(1)} fusion(bf16[512,16384]{1,0:T(8,128)(2,1)} %bitcast_dynamic-update-slice_fusion, bf16[768,8192]{0,1:T(8,128)(2,1)} %bitcast.89, bf16[768,8192]{0,1:T(8,128)(2,1)} %bitcast.97), kind=kOutput, calls=%fused_computation.11 | convolution fusion | flops 12935233536 | bytes 43515904 | tf_op jit(solution)/shard_map/dot_general | solution.py:86
  321.6 1.3 pad_maximum_fusion.3
  322.9 1.9 copy.38
  324.8 0.1 slice_select_fusion
  324.9 0.5 collective-permute-start.2
  325.4 41.5 %collective-permute-done.2 = f32[1,2,192,576]{3,2,1,0:T(8,128)S(1)} collective-permute-done((f32[1,2,192,576]{3,2,1,0:T(8,128)S(1)}, f32[1,2,192,576]{3,2,1,0:T(8,128)S(1)}, u32[]{:S(2)}, u32[]{:S(2)}) %collective-permute-start.2) | collective-permute-done | bytes 884768 | tf_op jit(solution)/shard_map/ppermute | solution.py:12
  366.9 0.2 select_add_fusion
  367.1 0.1 slice_select_fusion.1
  367.2 0.1 collective-permute-start.3
  367.2 14.7 %fusion.20 = f32[192,64,128]{2,0,1:T(8,128)} fusion(bf16[64,192,768]{2,1,0:T(8,128)(2,1)} %fusion.1, bf16[96,64,8,128]{3,2,1,0:T(8,128)(2,1)} %get-tuple-element.13), kind=kOutput, calls=%fused_computation.34 | convolution fusion | flops 2415919104 | bytes 37748736 | tf_op jit(solution)/shard_map/hij,jhd->ihd/dot_general | solution.py:69
  381.9 19.5 %collective-permute-done.3 = f32[1,1,192,576]{3,2,1,0:T(8,128)S(1)} collective-permute-done((f32[1,1,192,576]{3,2,1,0:T(8,128)S(1)}, f32[1,1,192,576]{3,2,1,0:T(8,128)S(1)}, u32[]{:S(2)}, u32[]{:S(2)}) %collective-permute-start.3) | collective-permute-done | bytes 442400 | tf_op jit(solution)/shard_map/ppermute | solution.py:12
  401.5 0.9 add_bitcast_fusion
  402.4 0.0 reduce-scatter.3.cloned.1.call-update
  402.4 9.4 convolution_bitcast_fusion
  411.9 8.9 maximum_multiply_fusion
  420.8 16.6 %copy.39 = f32[192,64,192]{2,1,0:T(8,128)} copy(f32[192,64,192]{2,0,1:T(8,128)} %maximum_multiply_fusion) | data formatting | bytes 18874368
  437.4 545.2 %reduce-scatter.5.cloned.1.call-done = f32[32,16384]{1,0:T(8,128)} async-done(((f32[512,16384]{1,0:T(8,128)}), f32[32,16384]{1,0:T(8,128)}) %reduce-scatter.5.cloned.1.call-update) | async-done | bytes 2097168 | tf_op jit(solution)/shard_map/reduce_scatter | solution.py:99
  982.7 1.7 slice_bitcast_fusion.2
  984.4 1.2 copy.48
  985.5 1.2 copy.47
  986.7 12.4 %reduce-scatter.3.cloned.1.call-done = f32[96,576]{1,0:T(8,128)} async-done(((f32[192,576]{1,0:T(8,128)}), f32[96,576]{1,0:T(8,128)}) %reduce-scatter.3.cloned.1.call-update) | async-done | bytes 221200 | tf_op jit(solution)/shard_map/reduce_scatter | solution.py:97
  (17 shorter events, 0.1 us)
Async XLA Ops:
  7.2 975.5 %reduce-scatter.5.cloned.1.call-start = ((), (), s32[]{:S(2)}) async-start(), calls=%async_computation.3 | async-start | bytes 35651584 | tf_op jit(solution)/shard_map/reduce_scatter | solution.py:99
  8.3 26.9 %collective-permute-start = (bf16[192,576]{0,1:T(8,128)(2,1)S(1)}, bf16[192,576]{0,1:T(8,128)(2,1)S(1)}, u32[]{:S(2)}, u32[]{:S(2)}) collective-permute-start(bf16[192,576]{0,1:T(8,128)(2,1)S(1)} %copy.25), channel_id=1, source_target_pairs={{0,2},{2,0},{4,6},{6,4},{8,10},{10,8},{12,14},{14,12},{16,18},{18,... | collective-permute-start | bytes 663560 | tf_op jit(solution)/shard_map/ppermute | solution.py:12
  35.4 38.1 %collective-permute-start.1 = (bf16[384,576]{0,1:T(8,128)(2,1)S(1)}, bf16[384,576]{0,1:T(8,128)(2,1)}, u32[]{:S(2)}, u32[]{:S(2)}) collective-permute-start(bf16[384,576]{0,1:T(8,128)(2,1)S(1)} %pad_maximum_fusion.4), channel_id=1, source_target_pairs={{0,4},{2,6},{4,0},{6,2},{8,12},{10,14},{12,8},{14,10},{16,20},{18,... | collective-permute-start | bytes 1327112 | tf_op jit(solution)/shard_map/ppermute | solution.py:12
  73.5 62.9 %copy-start = (bf16[192,64,64]{0,2,1:T(8,128)(2,1)}, bf16[192,64,64]{0,2,1:T(8,128)(2,1)S(1)}, u32[]{:S(2)}) copy-start(bf16[192,64,64]{0,2,1:T(8,128)(2,1)S(1)} %copy.42) | copy-start | bytes 4718596
  75.2 0.8 copy-start.5
  75.2 23.6 %copy-start.4 = (bf16[384,576]{0,1:T(8,128)(2,1)}, bf16[384,576]{0,1:T(8,128)(2,1)S(1)}, u32[]{:S(2)}) copy-start(bf16[384,576]{0,1:T(8,128)(2,1)S(1)} %get-tuple-element.16) | copy-start | bytes 1327108
  75.9 60.5 %copy-start.6 = (bf16[768,64,1]{0,1,2:T(8,128)(2,1)}, bf16[768,64,1]{0,1,2:T(8,128)(2,1)S(1)}, u32[]{:S(2)}) copy-start(bf16[768,64,1]{0,1,2:T(8,128)(2,1)S(1)} %fusion.29) | copy-start | bytes 294916
  165.6 22.5 %copy-start.3 = (bf16[192,64,128]{2,1,0:T(8,128)(2,1)S(1)}, bf16[192,64,128]{2,1,0:T(8,128)(2,1)}, u32[]{:S(2)}) copy-start(bf16[192,64,128]{2,1,0:T(8,128)(2,1)} %param.7) | copy-start | bytes 9437188
  221.1 25.5 %copy-start.2 = (bf16[192,64,128]{2,1,0:T(8,128)(2,1)S(1)}, bf16[192,64,128]{2,1,0:T(8,128)(2,1)}, u32[]{:S(2)}) copy-start(bf16[192,64,128]{2,1,0:T(8,128)(2,1)} %slice.42) | copy-start | bytes 9437188
  288.8 1.6 copy-start.1
  288.8 710.2 %reduce-scatter.3.cloned.1.call-start = ((), (), s32[]{:S(2)}) async-start(), calls=%async_computation.2 | async-start | bytes 737280 | tf_op jit(solution)/shard_map/reduce_scatter | solution.py:97
  324.9 42.0 %collective-permute-start.2 = (f32[1,2,192,576]{3,2,1,0:T(8,128)S(1)}, f32[1,2,192,576]{3,2,1,0:T(8,128)S(1)}, u32[]{:S(2)}, u32[]{:S(2)}) collective-permute-start(f32[1,2,192,576]{3,2,1,0:T(8,128)S(1)} %slice_select_fusion), channel_id=1, source_target_pairs={{0,4},{2,6},{4,0},{6,2},{8,12},{10,14},{12,8},{14,10},{16,20},{18,... | collective-permute-start | bytes 2654216 | tf_op jit(solution)/shard_map/ppermute | solution.py:12
  367.1 35.2 %copy-start.7 = (bf16[768,64,1]{0,1,2:T(8,128)(2,1)S(1)}, bf16[768,64,1]{0,1,2:T(8,128)(2,1)}, u32[]{:S(2)}) copy-start(bf16[768,64,1]{0,1,2:T(8,128)(2,1)} %copy-done.6) | copy-start | bytes 294916
  367.2 34.3 %collective-permute-start.3 = (f32[1,1,192,576]{3,2,1,0:T(8,128)S(1)}, f32[1,1,192,576]{3,2,1,0:T(8,128)S(1)}, u32[]{:S(2)}, u32[]{:S(2)}) collective-permute-start(f32[1,1,192,576]{3,2,1,0:T(8,128)S(1)} %slice_select_fusion.1), channel_id=1, source_target_pairs={{0,2},{2,0},{4,6},{6,4},{8,10},{10,8},{12,14},{14,12},{16,18},{18,... | collective-permute-start | bytes 1327112 | tf_op jit(solution)/shard_map/ppermute | solution.py:12
Sparse Core Ops, SparseCore 0:
  289.0 693.6 reduce-scatter.4
  985.5 13.5 reduce-scatter.2
where the time goes:
time: 1020 us; the launch traced here: 1010 us
  waiting for transfers between devices  619 us (61%)
  matrix products  228 us (22%)
  local copies, waits for them, and re-layouts  104 us (10%)
  other arithmetic  35.8 us (4%)
  between operations  14.7 us (1%)
    reduce_scatter x1, waiting for transfers between devices, per_device(): lax.psum_scatter(lax.dot_general(latent, key_value, (((0,), (0,)), ((), (...  545 us
    unnamed x24, local copies, waits for them, and re-layouts  69.5 us
    ppermute x4, waiting for transfers between devices, partner(): lax.ppermute(value, axis, [(i, i ^ 1 << apart) for i in range(lax.axis_si...  61.1 us
    sub x1, matrix products, per_device(): probs = jax.nn.softmax(scores, axis=-1)  29.1 us
    dot_general x1, matrix products, per_device(): jnp.einsum('ihd,jhd->hij', d_output, values_here, preferred_element_type=...  25.5 us
    dot_general x1, matrix products, per_device(): lax.dot_general(latent, key_value, (((0,), (0,)), ((), ())), preferred_el...  24.8 us
    concatenate x1, local copies, waits for them, and re-layouts, per_device(): jnp.concatenate([w_uk.reshape(latent_width, -1), w_uv.reshape(latent_widt...  23.9 us
    dot_general x1, matrix products, per_device(): jnp.dot(latent, weights, preferred_element_type=jnp.float32)  22.8 us
  transfers between devices with their start and end apart: 6, of which 4 were waited for; matrix products, arithmetic and copies ran while one was open for 15% of the time, Pallas kernels for 0%

commit v1 on v0

v1 whole, which is shorter than its diff:
```python
import functools
import math

import jax
import jax.numpy as jnp
from jax import lax
from jax.experimental import pallas as pl
from jax.experimental.pallas import tpu as pltpu
from jax.sharding import PartitionSpec as P


GROUP = 4
CHUNK_HEADS = 16
BF = jnp.bfloat16
F32 = jnp.float32


def flip_send(value, axis, mask):
    return lax.ppermute(value, axis, [(i, i ^ mask) for i in range(lax.axis_size(axis))])


def dot(a, b, ca, cb):
    return lax.dot_general(a, b, (((ca,), (cb,)), ((), ())), preferred_element_type=F32)


def by_head(block_ref, wide_ref, put):
    rows, heads, width = block_ref.shape
    lanes = wide_ref.shape[1]
    for at in range(0, width, lanes):
        n = min(lanes, width - at)
        piece = block_ref[:, :, at : at + n].astype(F32).reshape(rows * heads, n)
        wide_ref[: rows * heads, :n] = piece
        for h in range(heads):
            put(h, slice(at, at + n), wide_ref[pl.ds(h, rows, heads), :][:, :n].astype(BF))


def pair_kernel(first, width, nope, orders, scale, *refs):
    pos_ref, slots_ref, lat_t_ref, q_block, do_block, uk_block, uv_block = refs[:7]
    refs = refs[7:]
    if not first:
        lg_in, rg_in, _ = refs[:3]
        refs = refs[3:]
    lg_ref, rg_ref, dq_ref, keep_a_ref, send_a_ref, keep_b_ref, send_b_ref = refs[:7]
    lat_a_ref, lat_b_ref, w_ref, q_ref, do_ref, deep_ref = refs[7:]
    step = pl.program_id(0)
    per_block = dq_ref.shape[1] // 2
    at = step % per_block

    @pl.when(at == 0)
    def _():
        def put_q(h, lanes, x):
            q_ref[h, :, lanes] = x

        def put_do(h, lanes, x):
            do_ref[h, :, lanes] = x

        def put_uk(h, lanes, x):
            w_ref[h // 2, :, (h % 2) * nope : (h % 2 + 1) * nope] = x

        def put_uv(h, lanes, x):
            w_ref[h // 2, :, (2 + h % 2) * nope : (3 + h % 2) * nope] = x

        by_head(q_block, deep_ref, put_q)
        by_head(do_block, deep_ref, put_do)
        by_head(uk_block, deep_ref, put_uk)
        by_head(uv_block, deep_ref, put_uv)

    @pl.when(step == 0)
    def _():
        if first:
            lg_ref[...] = jnp.zeros_like(lg_ref)
            rg_ref[...] = jnp.zeros_like(rg_ref)
        else:
            lg_ref[...] = lg_in[...]
            rg_ref[...] = rg_in[...]
        position = pos_ref[0]
        for order, lat_ref in zip(orders, (lat_a_ref, lat_b_ref)):
            blocks = 1 << len(order)
            each = width // blocks
            for t in range(blocks):
                k = sum(((t >> (len(order) - 1 - n)) & 1) << bit for n, bit in enumerate(order))
                row = pl.multiple_of((position ^ k) * each, each)
                lat_ref[t * each : (t + 1) * each] = lat_t_ref[pl.ds(row, each), :]

    ukv = w_ref[at]
    kv = dot(slots_ref[:, :width], ukv, 1, 0).astype(BF)
    key_rope = slots_ref[:, width:]
    kcs, ss, gps = [], [], []
    for e in range(2):
        kcs.append(jnp.concatenate([kv[:, e * nope : (e + 1) * nope], key_rope], axis=1))
        ss.append(dot(kcs[e], q_ref[2 * at + e], 1, 1))
        gps.append(dot(kv[:, (2 + e) * nope : (3 + e) * nope], do_ref[2 * at + e], 1, 1))
    lows, dss = [], []
    for e in range(2):
        p = jnp.exp((ss[e] - jnp.max(ss[e], axis=0, keepdims=True)) * scale)
        p = p * (1.0 / jnp.sum(p, axis=0, keepdims=True))
        lows.append(p.astype(BF))
        delta = jnp.sum(lows[e].astype(F32) * gps[e], axis=0, keepdims=True)
        dss.append((p * (gps[e] - delta)).astype(BF))
    dks, dvs, dqs = [], [], []
    for e in range(2):
        dkc = dot(dss[e], q_ref[2 * at + e], 1, 0) * scale
        dvs.append(dot(lows[e], do_ref[2 * at + e], 1, 0).astype(BF))
        dks.append(dkc[:, :nope].astype(BF))
        rg_ref[...] += dkc[:, nope:]
        dqs.append(dot(dss[e], kcs[e], 0, 0) * scale)
    grads = jnp.concatenate(dks + dvs, axis=1)
    lg_ref[...] += dot(grads, ukv, 1, 1)
    half = keep_a_ref.shape[0]
    for at_w, (lat_ref, keep_ref, send_ref) in enumerate(
        ((lat_a_ref, keep_a_ref, send_a_ref), (lat_b_ref, keep_b_ref, send_b_ref))
    ):
        grad = grads[:, at_w * 2 * nope : (at_w + 1) * 2 * nope]
        dw = dot(lat_ref[...], grad, 1, 0).astype(BF)
        keep_ref[...] = dw[:half]
        send_ref[...] = dw[half:]
    for q in range(per_block):

        @pl.when(at == q)
        def _(q=q):
            for e in range(2):
                dq_ref[:, 2 * q + e, :] = dqs[e]


def chunk_sizes(heads):
    sizes = []
    left = heads
    while left > CHUNK_HEADS:
        sizes.append(CHUNK_HEADS)
        left -= CHUNK_HEADS
    if left % 16 == 0:
        return sizes + [left // 2, left // 2]
    return sizes + [left]


def per_device(compressed, query, d_output, w_uk, w_uv):
    rows = compressed.shape[0]
    width = w_uk.shape[0]
    heads = w_uk.shape[1]
    nope = w_uk.shape[2]
    rope = query.shape[2] - nope
    scale = 1.0 / math.sqrt(query.shape[2])
    ctx = lax.axis_size("ctx")
    bits = ctx.bit_length() - 1
    group_bits = GROUP.bit_length() - 1
    position = lax.axis_index("ctx")
    span = rows * GROUP
    slots = jnp.concatenate(
        [compressed] + [flip_send(compressed, "ctx", m) for m in range(1, GROUP)], axis=0
    )
    lat_t = jnp.transpose(slots[:, :width])
    rows_each = width // ctx
    far = list(range(group_bits, bits))
    orders = [[0, 1] + far, [1, 0] + far]
    params = pltpu.CompilerParams(
        dimension_semantics=("arbitrary",), vmem_limit_bytes=56 * 1024 * 1024
    )
    lg = rg = dq = None
    flows = []
    start = 0
    for c, chunk in enumerate(chunk_sizes(heads)):
        dq_heads = min(8, chunk)
        per_dq = dq_heads // 2
        first = c == 0
        whole = lambda shape: pl.BlockSpec(shape, lambda g: (0,) * len(shape))
        offset = start // dq_heads
        head_block = lambda n, w, offset=offset, per_dq=per_dq, dq_heads=dq_heads: pl.BlockSpec(
            (n, dq_heads, w), lambda g: (0, offset + g // per_dq, 0)
        )
        by_lane = lambda n, w: pl.BlockSpec((n, w), lambda g: (0, g))
        ins = [position.astype(jnp.int32).reshape(1), slots, lat_t, query, d_output, w_uk, w_uv]
        in_specs = [
            pl.BlockSpec(memory_space=pltpu.SMEM),
            whole((span, width + rope)),
            whole((width, span)),
            head_block(rows, nope + rope),
            head_block(rows, nope),
            head_block(width, nope),
            head_block(width, nope),
        ]
        alias = {}
        if not first:
            ins += [lg, rg, dq]
            in_specs += [
                whole((span, width)),
                whole((span, rope)),
                pl.BlockSpec(memory_space=pl.ANY),
            ]
            alias = {9: 2}
        half_spec = by_lane(width // 2, 2 * nope)
        half_shape = jax.ShapeDtypeStruct((width // 2, chunk * nope), BF)
        lg, rg, dq, keep_a, send_a, keep_b, send_b = pl.pallas_call(
            functools.partial(pair_kernel, first, width, nope, orders, scale),
            grid=(chunk // 2,),
            in_specs=in_specs,
            out_specs=[
                whole((span, width)),
                whole((span, rope)),
                head_block(rows, nope + rope),
                half_spec,
                half_spec,
                half_spec,
                half_spec,
            ],
            out_shape=[
                jax.ShapeDtypeStruct((span, width), F32),
                jax.ShapeDtypeStruct((span, rope), F32),
                jax.ShapeDtypeStruct((rows, heads, nope + rope), F32),
                half_shape,
                half_shape,
                half_shape,
                half_shape,
            ],
            scratch_shapes=[
                pltpu.VMEM((width, span), BF),
                pltpu.VMEM((width, span), BF),
                pltpu.VMEM((per_dq, width, 4 * nope), BF),
                pltpu.VMEM((dq_heads, rows, nope + rope), BF),
                pltpu.VMEM((dq_heads, rows, nope), BF),
                pltpu.VMEM((dq_heads * max(rows, width), nope), F32),
            ],
            input_output_aliases=alias,
            compiler_params=params,
        )(*ins)
        flows.append([(keep_a, send_a), (keep_b, send_b)])
        start += chunk

    grads = []
    for w, order in enumerate(orders):
        finals = []
        for flow in flows:
            keep, send = flow[w]
            for at_bit, bit in enumerate(order):
                came = flip_send(send, "ctx", 1 << bit)
                total = keep.astype(F32) + came.astype(F32)
                if at_bit == bits - 1:
                    finals.append(total)
                else:
                    total = total.astype(BF)
                    half = total.shape[0] // 2
                    keep, send = total[:half], total[half:]
        grads.append(jnp.concatenate(finals, axis=1).reshape(rows_each, heads, nope))

    partial = jnp.concatenate([lg, rg], axis=1)
    for bit in reversed(range(group_bits)):
        half = partial.shape[0] // 2
        partial = partial[:half] + flip_send(partial[half:].astype(BF), "ctx", 1 << bit).astype(F32)
    n_head = lax.axis_size("head")
    own = lax.axis_index("head")
    piece = rows // n_head
    cut = lambda i: lax.dynamic_slice_in_dim(partial, (i % n_head) * piece, piece, 0)
    d_compressed = cut(own)
    for r in range(1, n_head):
        d_compressed = d_compressed + lax.ppermute(
            cut(own + r), "head", [(i, (i + r) % n_head) for i in range(n_head)]
        )
    return (dq, d_compressed, *grads)


def solution(mesh):
    placed = (
        P("ctx", None),
        P("ctx", "head", None),
        P("ctx", "head", None),
        P(None, "head", None),
        P(None, "head", None),
    )

    return jax.shard_map(
        per_device,
        mesh=mesh,
        in_specs=placed,
        out_specs=(
            P("ctx", "head", None),
            P(("ctx", "head"), None),
            P("ctx", "head", None),
            P("ctx", "head", None),
        ),
        check_vma=False,
    )
```

time: 1020 us -> 446 us (0.44)
  waiting for transfers between devices: 619 us -> 212 us
  matrix products: 228 us -> 0 us
  Pallas kernels: 0 us -> 149 us
  local copies, waits for them, and re-layouts: 104 us -> 8.87 us
  starting transfers between devices: 5.24 us -> 59.8 us
  other arithmetic: 35.8 us -> 6.1 us
  between operations: 14.7 us -> 1.74 us
    reduce_scatter x2 -> x0, waiting for transfers between devices: 558 us -> none  [the longest x1 545 us: per_device(): lax.psum_scatter(lax.dot_general(latent, key_value, (((0,), (0,)), ((), (...]
    dot_general x11 -> x0, matrix products: 199 us -> none  [the longest x1 25.5 us: per_device(): jnp.einsum('ihd,jhd->hij', d_output, values_here, preferred_element_type=...]
    ppermute x4 -> x46, waiting for transfers between devices: 61.1 us -> 212 us  [the longest x45 211 us: flip_send(): lax.ppermute(value, axis, [(i, i ^ mask) for i in range(lax.axis_size(axi...]
    pallas_call x0 -> x5, Pallas kernels: none -> 149 us  [per_device(): pl.pallas_call(functools.partial(pair_kernel, first, width, nope, orders,...]
    unnamed x24 -> x36, local copies, waits for them, and re-layouts: 69.5 us -> 5.05 us
    ppermute x4 -> x46, starting transfers between devices: 5.16 us -> 59.8 us  [the longest x45 59.8 us: flip_send(): lax.ppermute(value, axis, [(i, i ^ mask) for i in range(lax.axis_size(axi...]
    sub x1 -> x0, matrix products: 29.1 us -> none  [per_device(): probs = jax.nn.softmax(scores, axis=-1)]
    concatenate x2, local copies, waits for them, and re-layouts: 25.7 us -> 1.37 us  [the longest x1 1.34 us: per_device(): jnp.concatenate([compressed] + [flip_send(compressed, 'ctx', m) for m in...]
  transfers between devices with their start and end apart: 6 -> 46, of which waited for: 4 -> 34; matrix products, arithmetic and copies ran while one was open for 15% -> 2% of each run, Pallas kernels for 0% -> 0%
where the time goes in v1:
time: 446 us; the launch traced here: 437 us
  waiting for transfers between devices  212 us (48%)
  Pallas kernels  149 us (33%)
  starting transfers between devices  59.8 us (13%)
  local copies, waits for them, and re-layouts  8.87 us (2%)
  other arithmetic  6.1 us (1%)
    ppermute x45, waiting for transfers between devices, flip_send(): lax.ppermute(value, axis, [(i, i ^ mask) for i in range(lax.axis_size(axi...  211 us
    pallas_call x5, Pallas kernels, per_device(): pl.pallas_call(functools.partial(pair_kernel, first, width, nope, orders,...  149 us
    ppermute x45, starting transfers between devices, flip_send(): lax.ppermute(value, axis, [(i, i ^ mask) for i in range(lax.axis_size(axi...  59.8 us
  transfers between devices with their start and end apart: 46, of which 34 were waited for; matrix products, arithmetic and copies ran while one was open for 2% of the time, Pallas kernels for 0%

profile of v1, /device:TPU:0, one launch (start us, length us, event | category | flops | bytes accessed | tf_op | source)
XLA Modules:
  0.0 437.3 jit_solution(11024688836363713998)
XLA Ops:
  1.7 4.0 collective-permute-start.2
  6.4 7.3 %collective-permute-done.2 = bf16[192,576]{0,1:T(8,128)(2,1)S(1)} collective-permute-done((bf16[192,576]{0,1:T(8,128)(2,1)S(1)}, bf16[192,576]{0,1:T(8,128)(2,1)S(1)}, u32[]{:S(2)}, u32[]{:S(2)}) %collective-permute-start.2) | collective-permute-done | bytes 221216 | tf_op jit(solution)/shard_map/ppermute | solution.py:19
  13.6 5.4 %collective-permute-done.1 = bf16[192,576]{0,1:T(8,128)(2,1)S(1)} collective-permute-done((bf16[192,576]{0,1:T(8,128)(2,1)S(1)}, bf16[192,576]{0,1:T(8,128)(2,1)S(1)}, u32[]{:S(2)}, u32[]{:S(2)}) %collective-permute-start.1) | collective-permute-done | bytes 221216 | tf_op jit(solution)/shard_map/ppermute | solution.py:19
  22.0 35.2 %shard_map.84 = (f32[768,512]{1,0:T(8,128)}, f32[768,64]{1,0:T(8,128)}, f32[192,64,192]{2,1,0:T(8,128)}, bf16[256,2048]{1,0:T(8,128)(2,1)}, bf16[256,2048]{1,0:T...) custom-call(s32[1]{0:T(128)} %bitcast.refs_0_, bf16[768,576]{1,0:T(8,128)(2,1)} %copy.21.refs_1_, ...), custom_call_target="tpu_custom_call" | custom-call | tf_op jit(solution)/shard_map/pallas_call | solution.py:192
  57.2 35.9 %shard_map.85 = (f32[768,512]{1,0:T(8,128)}, f32[768,64]{1,0:T(8,128)}, f32[192,64,192]{2,1,0:T(8,128)}, bf16[256,2048]{1,0:T(8,128)(2,1)}, bf16[256,2048]{1,0:T...) custom-call(s32[1]{0:T(128)} %bitcast.refs_0_, ...), custom_call_target="tpu_custom_call", output_to_operand_aliasing={{2}: (9, {})} | custom-call | tf_op jit(solution)/shard_map/pallas_call | solution.py:192
  93.1 36.1 %shard_map.86 = (f32[768,512]{1,0:T(8,128)}, f32[768,64]{1,0:T(8,128)}, f32[192,64,192]{2,1,0:T(8,128)}, bf16[256,2048]{1,0:T(8,128)(2,1)}, bf16[256,2048]{1,0:T...) custom-call(s32[1]{0:T(128)} %bitcast.refs_0_, ...), custom_call_target="tpu_custom_call", output_to_operand_aliasing={{2}: (9, {})} | custom-call | tf_op jit(solution)/shard_map/pallas_call | solution.py:192
  129.2 20.6 %shard_map.87 = (f32[768,512]{1,0:T(8,128)}, f32[768,64]{1,0:T(8,128)}, f32[192,64,192]{2,1,0:T(8,128)}, bf16[256,1024]{1,0:T(8,128)(2,1)}, bf16[256,1024]{1,0:T...) custom-call(s32[1]{0:T(128)} %bitcast.refs_0_, ...), custom_call_target="tpu_custom_call", output_to_operand_aliasing={{2}: (9, {})} | custom-call | tf_op jit(solution)/shard_map/pallas_call | solution.py:192
  149.8 20.8 %shard_map.88 = (f32[768,512]{1,0:T(8,128)}, f32[768,64]{1,0:T(8,128)}, f32[192,64,192]{2,1,0:T(8,128)}, bf16[256,1024]{1,0:T(8,128)(2,1)}, bf16[256,1024]{1,0:T...) custom-call(s32[1]{0:T(128)} %bitcast.refs_0_, ...), custom_call_target="tpu_custom_call", output_to_operand_aliasing={{2}: (9, {})} | custom-call | tf_op jit(solution)/shard_map/pallas_call | solution.py:192
  178.7 8.8 %collective-permute-done.3 = bf16[384,576]{1,0:T(8,128)(2,1)S(1)} collective-permute-done((bf16[384,576]{1,0:T(8,128)(2,1)}, bf16[384,576]{1,0:T(8,128)(2,1)S(1)}, u32[]{:S(2)}, u32[]{:S(2)}) %collective-permute-start.3) | collective-permute-done | bytes 442400 | tf_op jit(solution)/shard_map/ppermute | solution.py:19
  190.5 29.4 %collective-permute-done.42 = bf16[256,1024]{1,0:T(8,128)(2,1)S(1)} collective-permute-done((bf16[256,1024]{1,0:T(8,128)(2,1)}, bf16[256,1024]{1,0:T(8,128)(2,1)S(1)}, u32[]{:S(2)}, u32[]{:S(2)}) %collective-permute-start.42) | collective-permute-done | bytes 524320 | tf_op jit(solution)/shard_map/ppermute | solution.py:19
  220.0 1.7 collective-permute-start.38
  221.9 22.7 %collective-permute-done.18 = bf16[256,1024]{1,0:T(8,128)(2,1)S(1)} collective-permute-done((bf16[256,1024]{1,0:T(8,128)(2,1)S(1)}, bf16[256,1024]{1,0:T(8,128)(2,1)S(1)}, u32[]{:S(2)}, u32[]{:S(2)}) %collective-permute-start.18) | collective-permute-done | bytes 524320 | tf_op jit(solution)/shard_map/ppermute | solution.py:19
  245.1 1.8 collective-permute-start.23
  247.1 4.2 collective-permute-done.4
  253.7 4.6 %collective-permute-done.43 = bf16[128,1024]{1,0:T(8,128)(2,1)S(1)} collective-permute-done((bf16[128,1024]{1,0:T(8,128)(2,1)S(1)}, bf16[128,1024]{1,0:T(8,128)(2,1)S(1)}, u32[]{:S(2)}, u32[]{:S(2)}) %collective-permute-start.43) | collective-permute-done | bytes 262176 | tf_op jit(solution)/shard_map/ppermute | solution.py:19
  258.8 1.7 collective-permute-start.30
  260.7 3.9 collective-permute-done.39
  268.4 3.2 collective-permute-done.24
  273.3 3.3 collective-permute-done.44
  278.2 3.3 collective-permute-done.20
  283.2 3.3 collective-permute-done.40
  286.9 1.8 collective-permute-start.34
  289.1 2.7 collective-permute-start.25
  293.5 2.3 collective-permute-start.21
  296.2 13.0 %collective-permute-done.14 = bf16[256,2048]{1,0:T(8,128)(2,1)S(1)} collective-permute-done((bf16[256,2048]{1,0:T(8,128)(2,1)S(1)}, bf16[256,2048]{1,0:T(8,128)(2,1)S(1)}, u32[]{:S(2)}, u32[]{:S(2)}) %collective-permute-start.14) | collective-permute-done | bytes 1048608 | tf_op jit(solution)/shard_map/ppermute | solution.py:19
  310.6 2.8 collective-permute-start.27
  313.9 6.0 %collective-permute-done.7 = bf16[128,2048]{1,0:T(8,128)(2,1)S(1)} collective-permute-done((bf16[128,2048]{1,0:T(8,128)(2,1)S(1)}, bf16[128,2048]{1,0:T(8,128)(2,1)S(1)}, u32[]{:S(2)}, u32[]{:S(2)}) %collective-permute-start.7) | collective-permute-done | bytes 524320 | tf_op jit(solution)/shard_map/ppermute | solution.py:19
  319.9 1.7 collective-permute-start.11
  321.7 2.5 collective-permute-start.31
  324.3 7.7 %collective-permute-done.11 = bf16[128,2048]{1,0:T(8,128)(2,1)S(1)} collective-permute-done((bf16[128,2048]{1,0:T(8,128)(2,1)S(1)}, bf16[128,2048]{1,0:T(8,128)(2,1)S(1)}, u32[]{:S(2)}, u32[]{:S(2)}) %collective-permute-start.11) | collective-permute-done | bytes 524320 | tf_op jit(solution)/shard_map/ppermute | solution.py:19
  332.0 1.7 collective-permute-start.15
  333.8 2.5 collective-permute-start.35
  336.5 5.3 %collective-permute-done.15 = bf16[128,2048]{1,0:T(8,128)(2,1)S(1)} collective-permute-done((bf16[128,2048]{1,0:T(8,128)(2,1)S(1)}, bf16[128,2048]{1,0:T(8,128)(2,1)S(1)}, u32[]{:S(2)}, u32[]{:S(2)}) %collective-permute-start.15) | collective-permute-done | bytes 524320 | tf_op jit(solution)/shard_map/ppermute | solution.py:19
  341.9 2.6 collective-permute-start.41
  344.6 1.6 collective-permute-start.8
  346.4 6.6 %collective-permute-done.8 = bf16[64,2048]{1,0:T(8,128)(2,1)S(1)} collective-permute-done((bf16[64,2048]{1,0:T(8,128)(2,1)S(1)}, bf16[64,2048]{1,0:T(8,128)(2,1)S(1)}, u32[]{:S(2)}, u32[]{:S(2)}) %collective-permute-start.8) | collective-permute-done | bytes 262176 | tf_op jit(solution)/shard_map/ppermute | solution.py:19
  354.7 5.8 %collective-permute-done.28 = bf16[64,2048]{1,0:T(8,128)(2,1)S(1)} collective-permute-done((bf16[64,2048]{1,0:T(8,128)(2,1)S(1)}, bf16[64,2048]{1,0:T(8,128)(2,1)S(1)}, u32[]{:S(2)}, u32[]{:S(2)}) %collective-permute-start.28) | collective-permute-done | bytes 262176 | tf_op jit(solution)/shard_map/ppermute | solution.py:19
  362.2 5.0 %collective-permute-done.12 = bf16[64,2048]{1,0:T(8,128)(2,1)S(1)} collective-permute-done((bf16[64,2048]{1,0:T(8,128)(2,1)S(1)}, bf16[64,2048]{1,0:T(8,128)(2,1)S(1)}, u32[]{:S(2)}, u32[]{:S(2)}) %collective-permute-start.12) | collective-permute-done | bytes 262176 | tf_op jit(solution)/shard_map/ppermute | solution.py:19
  368.8 5.7 %collective-permute-done.32 = bf16[64,2048]{1,0:T(8,128)(2,1)S(1)} collective-permute-done((bf16[64,2048]{1,0:T(8,128)(2,1)S(1)}, bf16[64,2048]{1,0:T(8,128)(2,1)S(1)}, u32[]{:S(2)}, u32[]{:S(2)}) %collective-permute-start.32) | collective-permute-done | bytes 262176 | tf_op jit(solution)/shard_map/ppermute | solution.py:19
  376.2 6.1 %collective-permute-done.16 = bf16[64,2048]{1,0:T(8,128)(2,1)S(1)} collective-permute-done((bf16[64,2048]{1,0:T(8,128)(2,1)S(1)}, bf16[64,2048]{1,0:T(8,128)(2,1)S(1)}, u32[]{:S(2)}, u32[]{:S(2)}) %collective-permute-start.16) | collective-permute-done | bytes 262176 | tf_op jit(solution)/shard_map/ppermute | solution.py:19
  383.9 5.7 %collective-permute-done.36 = bf16[64,2048]{1,0:T(8,128)(2,1)S(1)} collective-permute-done((bf16[64,2048]{1,0:T(8,128)(2,1)S(1)}, bf16[64,2048]{1,0:T(8,128)(2,1)S(1)}, u32[]{:S(2)}, u32[]{:S(2)}) %collective-permute-start.36) | collective-permute-done | bytes 262176 | tf_op jit(solution)/shard_map/ppermute | solution.py:19
  389.6 1.9 collective-permute-start.9
  391.7 5.2 %collective-permute-done.9 = bf16[32,2048]{1,0:T(8,128)(2,1)S(1)} collective-permute-done((bf16[32,2048]{1,0:T(8,128)(2,1)S(1)}, bf16[32,2048]{1,0:T(8,128)(2,1)S(1)}, u32[]{:S(2)}, u32[]{:S(2)}) %collective-permute-start.9) | collective-permute-done | bytes 131104 | tf_op jit(solution)/shard_map/ppermute | solution.py:19
  397.6 8.4 %collective-permute-done.29 = bf16[32,2048]{1,0:T(8,128)(2,1)S(1)} collective-permute-done((bf16[32,2048]{1,0:T(8,128)(2,1)S(1)}, bf16[32,2048]{1,0:T(8,128)(2,1)S(1)}, u32[]{:S(2)}, u32[]{:S(2)}) %collective-permute-start.29) | collective-permute-done | bytes 131104 | tf_op jit(solution)/shard_map/ppermute | solution.py:19
  406.0 8.5 %collective-permute-done.13 = bf16[32,2048]{1,0:T(8,128)(2,1)S(1)} collective-permute-done((bf16[32,2048]{1,0:T(8,128)(2,1)S(1)}, bf16[32,2048]{1,0:T(8,128)(2,1)S(1)}, u32[]{:S(2)}, u32[]{:S(2)}) %collective-permute-start.13) | collective-permute-done | bytes 131104 | tf_op jit(solution)/shard_map/ppermute | solution.py:19
  414.5 6.9 %collective-permute-done.33 = bf16[32,2048]{1,0:T(8,128)(2,1)S(1)} collective-permute-done((bf16[32,2048]{1,0:T(8,128)(2,1)S(1)}, bf16[32,2048]{1,0:T(8,128)(2,1)S(1)}, u32[]{:S(2)}, u32[]{:S(2)}) %collective-permute-start.33) | collective-permute-done | bytes 131104 | tf_op jit(solution)/shard_map/ppermute | solution.py:19
  421.5 6.9 %collective-permute-done.17 = bf16[32,2048]{1,0:T(8,128)(2,1)S(1)} collective-permute-done((bf16[32,2048]{1,0:T(8,128)(2,1)S(1)}, bf16[32,2048]{1,0:T(8,128)(2,1)S(1)}, u32[]{:S(2)}, u32[]{:S(2)}) %collective-permute-start.17) | collective-permute-done | bytes 131104 | tf_op jit(solution)/shard_map/ppermute | solution.py:19
  428.5 5.9 %collective-permute-done.37 = bf16[32,2048]{1,0:T(8,128)(2,1)S(1)} collective-permute-done((bf16[32,2048]{1,0:T(8,128)(2,1)S(1)}, bf16[32,2048]{1,0:T(8,128)(2,1)S(1)}, u32[]{:S(2)}, u32[]{:S(2)}) %collective-permute-start.37) | collective-permute-done | bytes 131104 | tf_op jit(solution)/shard_map/ppermute | solution.py:19
  (165 shorter events, 45.5 us)
Async XLA Ops:
  1.7 11.9 %collective-permute-start.2 = (bf16[192,576]{0,1:T(8,128)(2,1)S(1)}, bf16[192,576]{0,1:T(8,128)(2,1)S(1)}, u32[]{:S(2)}, u32[]{:S(2)}) collective-permute-start(bf16[192,576]{0,1:T(8,128)(2,1)S(1)} %copy.16), channel_id=1, source_target_pairs={{0,6},{2,4},{4,2},{6,0},{8,14},{10,12},{12,10},{14,8},{16,22},{18,... | collective-permute-start | bytes 663560 | tf_op jit(solution)/shard_map/ppermute | solution.py:19
  5.7 13.3 %collective-permute-start.1 = (bf16[192,576]{0,1:T(8,128)(2,1)S(1)}, bf16[192,576]{0,1:T(8,128)(2,1)S(1)}, u32[]{:S(2)}, u32[]{:S(2)}) collective-permute-start(bf16[192,576]{0,1:T(8,128)(2,1)S(1)} %copy.16), channel_id=1, source_target_pairs={{0,4},{2,6},{4,0},{6,2},{8,12},{10,14},{12,8},{14,10},{16,20},{18,... | collective-permute-start | bytes 663560 | tf_op jit(solution)/shard_map/ppermute | solution.py:19
  6.2 13.1 %collective-permute-start = (bf16[192,576]{0,1:T(8,128)(2,1)S(1)}, bf16[192,576]{0,1:T(8,128)(2,1)S(1)}, u32[]{:S(2)}, u32[]{:S(2)}) collective-permute-start(bf16[192,576]{0,1:T(8,128)(2,1)S(1)} %copy.16), channel_id=1, source_target_pairs={{0,2},{2,0},{4,6},{6,4},{8,10},{10,8},{12,14},{14,12},{16,18},{18,... | collective-permute-start | bytes 663560 | tf_op jit(solution)/shard_map/ppermute | solution.py:19
  173.2 14.3 %collective-permute-start.3 = (bf16[384,576]{1,0:T(8,128)(2,1)}, bf16[384,576]{1,0:T(8,128)(2,1)S(1)}, u32[]{:S(2)}, u32[]{:S(2)}) collective-permute-start(bf16[384,576]{1,0:T(8,128)(2,1)} %slice.362), channel_id=1, source_target_pairs={{0,4},{2,6},{4,0},{6,2},{8,12},{10,14},{12,8},{14,10},{16,20},{18,... | collective-permute-start | bytes 1327112 | tf_op jit(solution)/shard_map/ppermute | solution.py:19
  174.6 15.0 %collective-permute-start.22 = (bf16[256,1024]{1,0:T(8,128)(2,1)}, bf16[256,1024]{1,0:T(8,128)(2,1)S(1)}, u32[]{:S(2)}, u32[]{:S(2)}) collective-permute-start(bf16[256,1024]{1,0:T(8,128)(2,1)} %get-tuple-element.63), channel_id=1, source_target_pairs={{0,2},{2,0},{4,6},{6,4},{8,10},{10,8},{12,14},{14,12},{16,18},{18,... | collective-permute-start | bytes 1572872 | tf_op jit(solution)/shard_map/ppermute | solution.py:19
  175.3 111.6 %collective-permute-start.6 = (bf16[256,2048]{1,0:T(8,128)(2,1)}, bf16[256,2048]{1,0:T(8,128)(2,1)S(1)}, u32[]{:S(2)}, u32[]{:S(2)}) collective-permute-start(bf16[256,2048]{1,0:T(8,128)(2,1)} %get-tuple-element.55), channel_id=1, source_target_pairs={{0,2},{2,0},{4,6},{6,4},{8,10},{10,8},{12,14},{14,12},{16,18},{18,... | collective-permute-start | bytes 3145736 | tf_op jit(solution)/shard_map/ppermute | solution.py:19
  176.6 112.5 %collective-permute-start.26 = (bf16[256,2048]{1,0:T(8,128)(2,1)}, bf16[256,2048]{1,0:T(8,128)(2,1)S(1)}, u32[]{:S(2)}, u32[]{:S(2)}) collective-permute-start(bf16[256,2048]{1,0:T(8,128)(2,1)} %get-tuple-element.65), channel_id=1, source_target_pairs={{0,4},{2,6},{4,0},{6,2},{8,12},{10,14},{12,8},{14,10},{16,20},{18,... | collective-permute-start | bytes 3145736 | tf_op jit(solution)/shard_map/ppermute | solution.py:19
  177.2 115.0 %collective-permute-start.10 = (bf16[256,2048]{1,0:T(8,128)(2,1)}, bf16[256,2048]{1,0:T(8,128)(2,1)S(1)}, u32[]{:S(2)}, u32[]{:S(2)}) collective-permute-start(bf16[256,2048]{1,0:T(8,128)(2,1)} %get-tuple-element.57), channel_id=1, source_target_pairs={{0,2},{2,0},{4,6},{6,4},{8,10},{10,8},{12,14},{14,12},{16,18},{18,... | collective-permute-start | bytes 3145736 | tf_op jit(solution)/shard_map/ppermute | solution.py:19
  187.5 34.2 %copy-start.8 = (bf16[256,1024]{1,0:T(8,128)(2,1)S(1)}, bf16[256,1024]{1,0:T(8,128)(2,1)}, u32[]{:S(2)}) copy-start(bf16[256,1024]{1,0:T(8,128)(2,1)} %get-tuple-element.72) | copy-start | bytes 1572868
  187.5 32.5 %collective-permute-start.42 = (bf16[256,1024]{1,0:T(8,128)(2,1)}, bf16[256,1024]{1,0:T(8,128)(2,1)S(1)}, u32[]{:S(2)}, u32[]{:S(2)}) collective-permute-start(bf16[256,1024]{1,0:T(8,128)(2,1)} %get-tuple-element.73), channel_id=1, source_target_pairs={{0,4},{2,6},{4,0},{6,2},{8,12},{10,14},{12,8},{14,10},{16,20},{18,... | collective-permute-start | bytes 1572872 | tf_op jit(solution)/shard_map/ppermute | solution.py:19
  189.6 55.0 %collective-permute-start.18 = (bf16[256,1024]{1,0:T(8,128)(2,1)S(1)}, bf16[256,1024]{1,0:T(8,128)(2,1)S(1)}, u32[]{:S(2)}, u32[]{:S(2)}) collective-permute-start(bf16[256,1024]{1,0:T(8,128)(2,1)S(1)} %copy-done.15), channel_id=1, source_target_pairs={{0,2},{2,0},{4,6},{6,4},{8,10},{10,8},{12,14},{14,12},{16,18},{18,... | collective-permute-start | bytes 1572872 | tf_op jit(solution)/shard_map/ppermute | solution.py:19
  190.3 54.6 %copy-start.7 = (bf16[256,1024]{1,0:T(8,128)(2,1)S(1)}, bf16[256,1024]{1,0:T(8,128)(2,1)}, u32[]{:S(2)}) copy-start(bf16[256,1024]{1,0:T(8,128)(2,1)} %get-tuple-element.60) | copy-start | bytes 1572868
  220.0 25.1 %collective-permute-start.38 = (bf16[256,1024]{1,0:T(8,128)(2,1)S(1)}, bf16[256,1024]{1,0:T(8,128)(2,1)S(1)}, u32[]{:S(2)}, u32[]{:S(2)}) collective-permute-start(bf16[256,1024]{1,0:T(8,128)(2,1)S(1)} %copy-done.14), channel_id=1, source_target_pairs={{0,4},{2,6},{4,0},{6,2},{8,12},{10,14},{12,8},{14,10},{16,20},{18,... | collective-permute-start | bytes 1572872 | tf_op jit(solution)/shard_map/ppermute | solution.py:19
  244.6 6.7 %collective-permute-start.4 = (bf16[192,576]{1,0:T(8,128)(2,1)S(1)}, bf16[192,576]{1,0:T(8,128)(2,1)S(1)}, u32[]{:S(2)}, u32[]{:S(2)}) collective-permute-start(bf16[192,576]{1,0:T(8,128)(2,1)S(1)} %slice.363), channel_id=1, source_target_pairs={{0,2},{2,0},{4,6},{6,4},{8,10},{10,8},{12,14},{14,12},{16,18},{18,... | collective-permute-start | bytes 663560 | tf_op jit(solution)/shard_map/ppermute | solution.py:19
  245.1 6.9 %collective-permute-start.23 = (bf16[128,1024]{1,0:T(8,128)(2,1)S(1)}, bf16[128,1024]{1,0:T(8,128)(2,1)S(1)}, u32[]{:S(2)}, u32[]{:S(2)}) collective-permute-start(bf16[128,1024]{1,0:T(8,128)(2,1)S(1)} %slice.292), channel_id=1, source_target_pairs={{0,4},{2,6},{4,0},{6,2},{8,12},{10,14},{12,8},{14,10},{16,20},{18,... | collective-permute-start | bytes 786440 | tf_op jit(solution)/shard_map/ppermute | solution.py:19
  251.3 6.9 %collective-permute-start.43 = (bf16[128,1024]{1,0:T(8,128)(2,1)S(1)}, bf16[128,1024]{1,0:T(8,128)(2,1)S(1)}, u32[]{:S(2)}, u32[]{:S(2)}) collective-permute-start(bf16[128,1024]{1,0:T(8,128)(2,1)S(1)} %slice.322), channel_id=1, source_target_pairs={{0,2},{2,0},{4,6},{6,4},{8,10},{10,8},{12,14},{14,12},{16,18},{18,... | collective-permute-start | bytes 786440 | tf_op jit(solution)/shard_map/ppermute | solution.py:19
  252.0 6.9 %collective-permute-start.19 = (bf16[128,1024]{1,0:T(8,128)(2,1)S(1)}, bf16[128,1024]{1,0:T(8,128)(2,1)S(1)}, u32[]{:S(2)}, u32[]{:S(2)}) collective-permute-start(bf16[128,1024]{1,0:T(8,128)(2,1)S(1)} %slice.286), channel_id=1, source_target_pairs={{0,4},{2,6},{4,0},{6,2},{8,12},{10,14},{12,8},{14,10},{16,20},{18,... | collective-permute-start | bytes 786440 | tf_op jit(solution)/shard_map/ppermute | solution.py:19
  258.2 6.4 %collective-permute-start.39 = (bf16[128,1024]{1,0:T(8,128)(2,1)S(1)}, bf16[128,1024]{1,0:T(8,128)(2,1)S(1)}, u32[]{:S(2)}, u32[]{:S(2)}) collective-permute-start(bf16[128,1024]{1,0:T(8,128)(2,1)S(1)} %slice.316), channel_id=1, source_target_pairs={{0,2},{2,0},{4,6},{6,4},{8,10},{10,8},{12,14},{14,12},{16,18},{18,... | collective-permute-start | bytes 786440 | tf_op jit(solution)/shard_map/ppermute | solution.py:19
  258.8 34.6 %collective-permute-start.30 = (bf16[256,2048]{1,0:T(8,128)(2,1)S(1)}, bf16[256,2048]{1,0:T(8,128)(2,1)S(1)}, u32[]{:S(2)}, u32[]{:S(2)}) collective-permute-start(bf16[256,2048]{1,0:T(8,128)(2,1)S(1)} %copy-done.13), channel_id=1, source_target_pairs={{0,4},{2,6},{4,0},{6,2},{8,12},{10,14},{12,8},{14,10},{16,20},{18,... | collective-permute-start | bytes 3145736 | tf_op jit(solution)/shard_map/ppermute | solution.py:19
  264.6 1.5 collective-permute-start.5
  266.1 5.5 %collective-permute-start.24 = (bf16[64,1024]{1,0:T(8,128)(2,1)S(1)}, bf16[64,1024]{1,0:T(8,128)(2,1)S(1)}, u32[]{:S(2)}, u32[]{:S(2)}) collective-permute-start(bf16[64,1024]{1,0:T(8,128)(2,1)S(1)} %slice.294), channel_id=1, source_target_pairs={{0,8},{2,10},{4,12},{6,14},{8,0},{10,2},{12,4},{14,6},{16,24},{18,... | collective-permute-start | bytes 393224 | tf_op jit(solution)/shard_map/ppermute | solution.py:19
  271.6 5.0 %collective-permute-start.44 = (bf16[64,1024]{1,0:T(8,128)(2,1)S(1)}, bf16[64,1024]{1,0:T(8,128)(2,1)S(1)}, u32[]{:S(2)}, u32[]{:S(2)}) collective-permute-start(bf16[64,1024]{1,0:T(8,128)(2,1)S(1)} %slice.324), channel_id=1, source_target_pairs={{0,8},{2,10},{4,12},{6,14},{8,0},{10,2},{12,4},{14,6},{16,24},{18,... | collective-permute-start | bytes 393224 | tf_op jit(solution)/shard_map/ppermute | solution.py:19
  276.6 5.0 %collective-permute-start.20 = (bf16[64,1024]{1,0:T(8,128)(2,1)S(1)}, bf16[64,1024]{1,0:T(8,128)(2,1)S(1)}, u32[]{:S(2)}, u32[]{:S(2)}) collective-permute-start(bf16[64,1024]{1,0:T(8,128)(2,1)S(1)} %slice.288), channel_id=1, source_target_pairs={{0,8},{2,10},{4,12},{6,14},{8,0},{10,2},{12,4},{14,6},{16,24},{18,... | collective-permute-start | bytes 393224 | tf_op jit(solution)/shard_map/ppermute | solution.py:19
  281.6 5.0 %collective-permute-start.40 = (bf16[64,1024]{1,0:T(8,128)(2,1)S(1)}, bf16[64,1024]{1,0:T(8,128)(2,1)S(1)}, u32[]{:S(2)}, u32[]{:S(2)}) collective-permute-start(bf16[64,1024]{1,0:T(8,128)(2,1)S(1)} %slice.318), channel_id=1, source_target_pairs={{0,8},{2,10},{4,12},{6,14},{8,0},{10,2},{12,4},{14,6},{16,24},{18,... | collective-permute-start | bytes 393224 | tf_op jit(solution)/shard_map/ppermute | solution.py:19
  286.5 22.6 %collective-permute-start.14 = (bf16[256,2048]{1,0:T(8,128)(2,1)S(1)}, bf16[256,2048]{1,0:T(8,128)(2,1)S(1)}, u32[]{:S(2)}, u32[]{:S(2)}) collective-permute-start(bf16[256,2048]{1,0:T(8,128)(2,1)S(1)} %copy-done.12), channel_id=1, source_target_pairs={{0,2},{2,0},{4,6},{6,4},{8,10},{10,8},{12,14},{14,12},{16,18},{18,... | collective-permute-start | bytes 3145736 | tf_op jit(solution)/shard_map/ppermute | solution.py:19
  286.9 23.7 %collective-permute-start.34 = (bf16[256,2048]{1,0:T(8,128)(2,1)S(1)}, bf16[256,2048]{1,0:T(8,128)(2,1)S(1)}, u32[]{:S(2)}, u32[]{:S(2)}) collective-permute-start(bf16[256,2048]{1,0:T(8,128)(2,1)S(1)} %copy-done.11), channel_id=1, source_target_pairs={{0,4},{2,6},{4,0},{6,2},{8,12},{10,14},{12,8},{14,10},{16,20},{18,... | collective-permute-start | bytes 3145736 | tf_op jit(solution)/shard_map/ppermute | solution.py:19
  289.1 145.3 %collective-permute-start.25 = (bf16[32,1024]{1,0:T(8,128)(2,1)S(1)}, bf16[32,1024]{1,0:T(8,128)(2,1)S(1)}, u32[]{:S(2)}, u32[]{:S(2)}) collective-permute-start(bf16[32,1024]{1,0:T(8,128)(2,1)S(1)} %slice.296), channel_id=1, source_target_pairs={{0,16},{2,18},{4,20},{6,22},{8,24},{10,26},{12,28},{14,30},{16,0},... | collective-permute-start | bytes 196616 | tf_op jit(solution)/shard_map/ppermute | solution.py:19
  292.3 143.4 %collective-permute-start.45 = (bf16[32,1024]{1,0:T(8,128)(2,1)S(1)}, bf16[32,1024]{1,0:T(8,128)(2,1)S(1)}, u32[]{:S(2)}, u32[]{:S(2)}) collective-permute-start(bf16[32,1024]{1,0:T(8,128)(2,1)S(1)} %slice.326), channel_id=1, source_target_pairs={{0,16},{2,18},{4,20},{6,22},{8,24},{10,26},{12,28},{14,30},{16,0},... | collective-permute-start | bytes 196616 | tf_op jit(solution)/shard_map/ppermute | solution.py:19
  293.5 141.0 %collective-permute-start.21 = (bf16[32,1024]{1,0:T(8,128)(2,1)S(1)}, bf16[32,1024]{1,0:T(8,128)(2,1)S(1)}, u32[]{:S(2)}, u32[]{:S(2)}) collective-permute-start(bf16[32,1024]{1,0:T(8,128)(2,1)S(1)} %slice.290), channel_id=1, source_target_pairs={{0,16},{2,18},{4,20},{6,22},{8,24},{10,26},{12,28},{14,30},{16,0},... | collective-permute-start | bytes 196616 | tf_op jit(solution)/shard_map/ppermute | solution.py:19
  309.1 10.8 %collective-permute-start.7 = (bf16[128,2048]{1,0:T(8,128)(2,1)S(1)}, bf16[128,2048]{1,0:T(8,128)(2,1)S(1)}, u32[]{:S(2)}, u32[]{:S(2)}) collective-permute-start(bf16[128,2048]{1,0:T(8,128)(2,1)S(1)} %slice.268), channel_id=1, source_target_pairs={{0,4},{2,6},{4,0},{6,2},{8,12},{10,14},{12,8},{14,10},{16,20},{18,... | collective-permute-start | bytes 1572872 | tf_op jit(solution)/shard_map/ppermute | solution.py:19
  310.6 11.1 %collective-permute-start.27 = (bf16[128,2048]{1,0:T(8,128)(2,1)S(1)}, bf16[128,2048]{1,0:T(8,128)(2,1)S(1)}, u32[]{:S(2)}, u32[]{:S(2)}) collective-permute-start(bf16[128,2048]{1,0:T(8,128)(2,1)S(1)} %slice.298), channel_id=1, source_target_pairs={{0,2},{2,0},{4,6},{6,4},{8,10},{10,8},{12,14},{14,12},{16,18},{18,... | collective-permute-start | bytes 1572872 | tf_op jit(solution)/shard_map/ppermute | solution.py:19
  319.9 12.1 %collective-permute-start.11 = (bf16[128,2048]{1,0:T(8,128)(2,1)S(1)}, bf16[128,2048]{1,0:T(8,128)(2,1)S(1)}, u32[]{:S(2)}, u32[]{:S(2)}) collective-permute-start(bf16[128,2048]{1,0:T(8,128)(2,1)S(1)} %slice.274), channel_id=1, source_target_pairs={{0,4},{2,6},{4,0},{6,2},{8,12},{10,14},{12,8},{14,10},{16,20},{18,... | collective-permute-start | bytes 1572872 | tf_op jit(solution)/shard_map/ppermute | solution.py:19
  321.7 12.1 %collective-permute-start.31 = (bf16[128,2048]{1,0:T(8,128)(2,1)S(1)}, bf16[128,2048]{1,0:T(8,128)(2,1)S(1)}, u32[]{:S(2)}, u32[]{:S(2)}) collective-permute-start(bf16[128,2048]{1,0:T(8,128)(2,1)S(1)} %slice.304), channel_id=1, source_target_pairs={{0,2},{2,0},{4,6},{6,4},{8,10},{10,8},{12,14},{14,12},{16,18},{18,... | collective-permute-start | bytes 1572872 | tf_op jit(solution)/shard_map/ppermute | solution.py:19
  332.0 9.9 %collective-permute-start.15 = (bf16[128,2048]{1,0:T(8,128)(2,1)S(1)}, bf16[128,2048]{1,0:T(8,128)(2,1)S(1)}, u32[]{:S(2)}, u32[]{:S(2)}) collective-permute-start(bf16[128,2048]{1,0:T(8,128)(2,1)S(1)} %slice.280), channel_id=1, source_target_pairs={{0,4},{2,6},{4,0},{6,2},{8,12},{10,14},{12,8},{14,10},{16,20},{18,... | collective-permute-start | bytes 1572872 | tf_op jit(solution)/shard_map/ppermute | solution.py:19
  333.8 10.8 %collective-permute-start.35 = (bf16[128,2048]{1,0:T(8,128)(2,1)S(1)}, bf16[128,2048]{1,0:T(8,128)(2,1)S(1)}, u32[]{:S(2)}, u32[]{:S(2)}) collective-permute-start(bf16[128,2048]{1,0:T(8,128)(2,1)S(1)} %slice.310), channel_id=1, source_target_pairs={{0,2},{2,0},{4,6},{6,4},{8,10},{10,8},{12,14},{14,12},{16,18},{18,... | collective-permute-start | bytes 1572872 | tf_op jit(solution)/shard_map/ppermute | solution.py:19
  341.9 92.6 %collective-permute-start.41 = (bf16[32,1024]{1,0:T(8,128)(2,1)S(1)}, bf16[32,1024]{1,0:T(8,128)(2,1)S(1)}, u32[]{:S(2)}, u32[]{:S(2)}) collective-permute-start(bf16[32,1024]{1,0:T(8,128)(2,1)S(1)} %slice.320), channel_id=1, source_target_pairs={{0,16},{2,18},{4,20},{6,22},{8,24},{10,26},{12,28},{14,30},{16,0},... | collective-permute-start | bytes 196616 | tf_op jit(solution)/shard_map/ppermute | solution.py:19
  344.6 8.4 %collective-permute-start.8 = (bf16[64,2048]{1,0:T(8,128)(2,1)S(1)}, bf16[64,2048]{1,0:T(8,128)(2,1)S(1)}, u32[]{:S(2)}, u32[]{:S(2)}) collective-permute-start(bf16[64,2048]{1,0:T(8,128)(2,1)S(1)} %slice.270), channel_id=1, source_target_pairs={{0,8},{2,10},{4,12},{6,14},{8,0},{10,2},{12,4},{14,6},{16,24},{18,... | collective-permute-start | bytes 786440 | tf_op jit(solution)/shard_map/ppermute | solution.py:19
  353.0 7.5 %collective-permute-start.28 = (bf16[64,2048]{1,0:T(8,128)(2,1)S(1)}, bf16[64,2048]{1,0:T(8,128)(2,1)S(1)}, u32[]{:S(2)}, u32[]{:S(2)}) collective-permute-start(bf16[64,2048]{1,0:T(8,128)(2,1)S(1)} %slice.300), channel_id=1, source_target_pairs={{0,8},{2,10},{4,12},{6,14},{8,0},{10,2},{12,4},{14,6},{16,24},{18,... | collective-permute-start | bytes 786440 | tf_op jit(solution)/shard_map/ppermute | solution.py:19
  360.5 6.6 %collective-permute-start.12 = (bf16[64,2048]{1,0:T(8,128)(2,1)S(1)}, bf16[64,2048]{1,0:T(8,128)(2,1)S(1)}, u32[]{:S(2)}, u32[]{:S(2)}) collective-permute-start(bf16[64,2048]{1,0:T(8,128)(2,1)S(1)} %slice.276), channel_id=1, source_target_pairs={{0,8},{2,10},{4,12},{6,14},{8,0},{10,2},{12,4},{14,6},{16,24},{18,... | collective-permute-start | bytes 786440 | tf_op jit(solution)/shard_map/ppermute | solution.py:19
  367.1 7.4 %collective-permute-start.32 = (bf16[64,2048]{1,0:T(8,128)(2,1)S(1)}, bf16[64,2048]{1,0:T(8,128)(2,1)S(1)}, u32[]{:S(2)}, u32[]{:S(2)}) collective-permute-start(bf16[64,2048]{1,0:T(8,128)(2,1)S(1)} %slice.306), channel_id=1, source_target_pairs={{0,8},{2,10},{4,12},{6,14},{8,0},{10,2},{12,4},{14,6},{16,24},{18,... | collective-permute-start | bytes 786440 | tf_op jit(solution)/shard_map/ppermute | solution.py:19
  374.5 7.8 %collective-permute-start.16 = (bf16[64,2048]{1,0:T(8,128)(2,1)S(1)}, bf16[64,2048]{1,0:T(8,128)(2,1)S(1)}, u32[]{:S(2)}, u32[]{:S(2)}) collective-permute-start(bf16[64,2048]{1,0:T(8,128)(2,1)S(1)} %slice.282), channel_id=1, source_target_pairs={{0,8},{2,10},{4,12},{6,14},{8,0},{10,2},{12,4},{14,6},{16,24},{18,... | collective-permute-start | bytes 786440 | tf_op jit(solution)/shard_map/ppermute | solution.py:19
  382.3 7.3 %collective-permute-start.36 = (bf16[64,2048]{1,0:T(8,128)(2,1)S(1)}, bf16[64,2048]{1,0:T(8,128)(2,1)S(1)}, u32[]{:S(2)}, u32[]{:S(2)}) collective-permute-start(bf16[64,2048]{1,0:T(8,128)(2,1)S(1)} %slice.312), channel_id=1, source_target_pairs={{0,8},{2,10},{4,12},{6,14},{8,0},{10,2},{12,4},{14,6},{16,24},{18,... | collective-permute-start | bytes 786440 | tf_op jit(solution)/shard_map/ppermute | solution.py:19
  389.6 7.3 %collective-permute-start.9 = (bf16[32,2048]{1,0:T(8,128)(2,1)S(1)}, bf16[32,2048]{1,0:T(8,128)(2,1)S(1)}, u32[]{:S(2)}, u32[]{:S(2)}) collective-permute-start(bf16[32,2048]{1,0:T(8,128)(2,1)S(1)} %slice.272), channel_id=1, source_target_pairs={{0,16},{2,18},{4,20},{6,22},{8,24},{10,26},{12,28},{14,30},{16,0},... | collective-permute-start | bytes 393224 | tf_op jit(solution)/shard_map/ppermute | solution.py:19
  396.9 9.1 %collective-permute-start.29 = (bf16[32,2048]{1,0:T(8,128)(2,1)S(1)}, bf16[32,2048]{1,0:T(8,128)(2,1)S(1)}, u32[]{:S(2)}, u32[]{:S(2)}) collective-permute-start(bf16[32,2048]{1,0:T(8,128)(2,1)S(1)} %slice.302), channel_id=1, source_target_pairs={{0,16},{2,18},{4,20},{6,22},{8,24},{10,26},{12,28},{14,30},{16,0},... | collective-permute-start | bytes 393224 | tf_op jit(solution)/shard_map/ppermute | solution.py:19
  406.0 8.5 %collective-permute-start.13 = (bf16[32,2048]{1,0:T(8,128)(2,1)S(1)}, bf16[32,2048]{1,0:T(8,128)(2,1)S(1)}, u32[]{:S(2)}, u32[]{:S(2)}) collective-permute-start(bf16[32,2048]{1,0:T(8,128)(2,1)S(1)} %slice.278), channel_id=1, source_target_pairs={{0,16},{2,18},{4,20},{6,22},{8,24},{10,26},{12,28},{14,30},{16,0},... | collective-permute-start | bytes 393224 | tf_op jit(solution)/shard_map/ppermute | solution.py:19
  414.5 7.0 %collective-permute-start.33 = (bf16[32,2048]{1,0:T(8,128)(2,1)S(1)}, bf16[32,2048]{1,0:T(8,128)(2,1)S(1)}, u32[]{:S(2)}, u32[]{:S(2)}) collective-permute-start(bf16[32,2048]{1,0:T(8,128)(2,1)S(1)} %slice.308), channel_id=1, source_target_pairs={{0,16},{2,18},{4,20},{6,22},{8,24},{10,26},{12,28},{14,30},{16,0},... | collective-permute-start | bytes 393224 | tf_op jit(solution)/shard_map/ppermute | solution.py:19
  421.5 7.0 %collective-permute-start.17 = (bf16[32,2048]{1,0:T(8,128)(2,1)S(1)}, bf16[32,2048]{1,0:T(8,128)(2,1)S(1)}, u32[]{:S(2)}, u32[]{:S(2)}) collective-permute-start(bf16[32,2048]{1,0:T(8,128)(2,1)S(1)} %slice.284), channel_id=1, source_target_pairs={{0,16},{2,18},{4,20},{6,22},{8,24},{10,26},{12,28},{14,30},{16,0},... | collective-permute-start | bytes 393224 | tf_op jit(solution)/shard_map/ppermute | solution.py:19
  428.4 6.0 %collective-permute-start.37 = (bf16[32,2048]{1,0:T(8,128)(2,1)S(1)}, bf16[32,2048]{1,0:T(8,128)(2,1)S(1)}, u32[]{:S(2)}, u32[]{:S(2)}) collective-permute-start(bf16[32,2048]{1,0:T(8,128)(2,1)S(1)} %slice.314), channel_id=1, source_target_pairs={{0,16},{2,18},{4,20},{6,22},{8,24},{10,26},{12,28},{14,30},{16,0},... | collective-permute-start | bytes 393224 | tf_op jit(solution)/shard_map/ppermute | solution.py:19
  (14 other events, 226.2 us)

commit v2 on v1

--- a/solution.py
+++ b/solution.py
@@ -25,13 +25,21 @@
 
 def by_head(block_ref, wide_ref, put):
     rows, heads, width = block_ref.shape
-    lanes = wide_ref.shape[1]
-    for at in range(0, width, lanes):
-        n = min(lanes, width - at)
-        piece = block_ref[:, :, at : at + n].astype(F32).reshape(rows * heads, n)
-        wide_ref[: rows * heads, :n] = piece
-        for h in range(heads):
-            put(h, slice(at, at + n), wide_ref[pl.ds(h, rows, heads), :][:, :n].astype(BF))
+    deep, lanes = wide_ref.shape
+    some = deep // heads
+
+    def move(r, carry):
+        row = pl.ds(pl.multiple_of(r * some, some), some)
+        for at in range(0, width, lanes):
+            n = min(lanes, width - at)
+            piece = block_ref[row, :, at : at + n].astype(F32).reshape(some * heads, n)
+            wide_ref[:, :n] = piece
+            for h in range(heads):
+                part = wide_ref[pl.ds(h, some, heads), :][:, :n].astype(BF)
+                put(h, row, slice(at, at + n), part)
+        return carry
+
+    lax.fori_loop(0, rows // some, move, 0)
 
 
 def pair_kernel(first, width, nope, orders, scale, *refs):
@@ -41,24 +49,24 @@
         lg_in, rg_in, _ = refs[:3]
         refs = refs[3:]
     lg_ref, rg_ref, dq_ref, keep_a_ref, send_a_ref, keep_b_ref, send_b_ref = refs[:7]
-    lat_a_ref, lat_b_ref, w_ref, q_ref, do_ref, deep_ref = refs[7:]
+    lat_a_ref, lat_b_ref, w_ref, q_ref, do_ref, deep_ref, dq_near_ref, dq_far_ref = refs[7:]
     step = pl.program_id(0)
     per_block = dq_ref.shape[1] // 2
     at = step % per_block
 
     @pl.when(at == 0)
     def _():
-        def put_q(h, lanes, x):
-            q_ref[h, :, lanes] = x
-
-        def put_do(h, lanes, x):
-            do_ref[h, :, lanes] = x
-
-        def put_uk(h, lanes, x):
-            w_ref[h // 2, :, (h % 2) * nope : (h % 2 + 1) * nope] = x
-
-        def put_uv(h, lanes, x):
-            w_ref[h // 2, :, (2 + h % 2) * nope : (3 + h % 2) * nope] = x
+        def put_q(h, row, lanes, x):
+            q_ref[h, row, lanes] = x
+
+        def put_do(h, row, lanes, x):
+            do_ref[h, row, lanes] = x
+
+        def put_uk(h, row, lanes, x):
+            w_ref[h // 2, row, (h % 2) * nope : (h % 2 + 1) * nope] = x
+
+        def put_uv(h, row, lanes, x):
+            w_ref[h // 2, row, (2 + h % 2) * nope : (3 + h % 2) * nope] = x
 
         by_head(q_block, deep_ref, put_q)
         by_head(do_block, deep_ref, put_do)
@@ -114,12 +122,18 @@
         dw = dot(lat_ref[...], grad, 1, 0).astype(BF)
         keep_ref[...] = dw[:half]
         send_ref[...] = dw[half:]
-    for q in range(per_block):
-
-        @pl.when(at == q)
-        def _(q=q):
-            for e in range(2):
-                dq_ref[:, 2 * q + e, :] = dqs[e]
+    rows, block_heads, deep = dq_ref.shape
+    for e in range(2):
+        spot = pl.ds(2 * at + e, rows, block_heads)
+        dq_near_ref[spot, :] = dqs[e][:, :nope]
+        dq_far_ref[spot, :] = jnp.concatenate(
+            [dqs[e][:, nope:], jnp.zeros((rows, 2 * nope - deep), F32)], axis=1
+        )
+
+    @pl.when(at == per_block - 1)
+    def _():
+        dq_ref[:, :, :nope] = dq_near_ref[...].reshape(rows, block_heads, nope)
+        dq_ref[:, :, nope:] = dq_far_ref[...].reshape(rows, block_heads, nope)[:, :, : deep - nope]
 
 
 def chunk_sizes(heads):
@@ -217,7 +231,9 @@
                 pltpu.VMEM((per_dq, width, 4 * nope), BF),
                 pltpu.VMEM((dq_heads, rows, nope + rope), BF),
                 pltpu.VMEM((dq_heads, rows, nope), BF),
-                pltpu.VMEM((dq_heads * max(rows, width), nope), F32),
+                pltpu.VMEM((dq_heads * math.gcd(rows, width), nope), F32),
+                pltpu.VMEM((dq_heads * rows, nope), F32),
+                pltpu.VMEM((dq_heads * rows, nope), F32),
             ],
             input_output_aliases=alias,
             compiler_params=params,

time: 446 us -> 432 us (0.969); the launches traced: 437 us -> 432 us
  Pallas kernels: 149 us -> 144 us
    pallas_call x5, Pallas kernels: 149 us -> 144 us  [per_device(): pl.pallas_call(functools.partial(pair_kernel, first, width, nope, orders,...]
where the time goes in v2:
time: 432 us
  waiting for transfers between devices  212 us (49%)
  Pallas kernels  144 us (33%)
  starting transfers between devices  59.8 us (14%)
  local copies, waits for them, and re-layouts  8.87 us (2%)
  other arithmetic  6.1 us (1%)
    ppermute x45, waiting for transfers between devices, flip_send(): lax.ppermute(value, axis, [(i, i ^ mask) for i in range(lax.axis_size(axi...  211 us
    pallas_call x5, Pallas kernels, per_device(): pl.pallas_call(functools.partial(pair_kernel, first, width, nope, orders,...  144 us
    ppermute x45, starting transfers between devices, flip_send(): lax.ppermute(value, axis, [(i, i ^ mask) for i in range(lax.axis_size(axi...  59.8 us
  transfers between devices with their start and end apart: 46, of which 34 were waited for; matrix products, arithmetic and copies ran while one was open for 2% of the time, Pallas kernels for 0%

profile of v2, /device:TPU:0, one launch (start us, length us, event | category | flops | bytes accessed | tf_op | source)
XLA Modules:
  0.0 432.3 jit_solution(16814773269529394792)
XLA Ops:
  1.7 4.0 collective-permute-start.2
  6.4 7.3 %collective-permute-done.2 = bf16[192,576]{0,1:T(8,128)(2,1)S(1)} collective-permute-done((bf16[192,576]{0,1:T(8,128)(2,1)S(1)}, bf16[192,576]{0,1:T(8,128)(2,1)S(1)}, u32[]{:S(2)}, u32[]{:S(2)}) %collective-permute-start.2) | collective-permute-done | bytes 221216 | tf_op jit(solution)/shard_map/ppermute | solution.py:19
  13.6 5.4 %collective-permute-done.1 = bf16[192,576]{0,1:T(8,128)(2,1)S(1)} collective-permute-done((bf16[192,576]{0,1:T(8,128)(2,1)S(1)}, bf16[192,576]{0,1:T(8,128)(2,1)S(1)}, u32[]{:S(2)}, u32[]{:S(2)}) %collective-permute-start.1) | collective-permute-done | bytes 221216 | tf_op jit(solution)/shard_map/ppermute | solution.py:19
  22.0 34.1 %shard_map.84 = (f32[768,512]{1,0:T(8,128)}, f32[768,64]{1,0:T(8,128)}, f32[192,64,192]{2,1,0:T(8,128)}, bf16[256,2048]{1,0:T(8,128)(2,1)}, bf16[256,2048]{1,0:T...) custom-call(s32[1]{0:T(128)} %bitcast.refs_0_, bf16[768,576]{1,0:T(8,128)(2,1)} %copy.21.refs_1_, ...), custom_call_target="tpu_custom_call" | custom-call | tf_op jit(solution)/shard_map/pallas_call | solution.py:206
  56.1 34.8 %shard_map.85 = (f32[768,512]{1,0:T(8,128)}, f32[768,64]{1,0:T(8,128)}, f32[192,64,192]{2,1,0:T(8,128)}, bf16[256,2048]{1,0:T(8,128)(2,1)}, bf16[256,2048]{1,0:T...) custom-call(s32[1]{0:T(128)} %bitcast.refs_0_, ...), custom_call_target="tpu_custom_call", output_to_operand_aliasing={{2}: (9, {})} | custom-call | tf_op jit(solution)/shard_map/pallas_call | solution.py:206
  90.9 34.8 %shard_map.86 = (f32[768,512]{1,0:T(8,128)}, f32[768,64]{1,0:T(8,128)}, f32[192,64,192]{2,1,0:T(8,128)}, bf16[256,2048]{1,0:T(8,128)(2,1)}, bf16[256,2048]{1,0:T...) custom-call(s32[1]{0:T(128)} %bitcast.refs_0_, ...), custom_call_target="tpu_custom_call", output_to_operand_aliasing={{2}: (9, {})} | custom-call | tf_op jit(solution)/shard_map/pallas_call | solution.py:206
  125.7 20.3 %shard_map.87 = (f32[768,512]{1,0:T(8,128)}, f32[768,64]{1,0:T(8,128)}, f32[192,64,192]{2,1,0:T(8,128)}, bf16[256,1024]{1,0:T(8,128)(2,1)}, bf16[256,1024]{1,0:T...) custom-call(s32[1]{0:T(128)} %bitcast.refs_0_, ...), custom_call_target="tpu_custom_call", output_to_operand_aliasing={{2}: (9, {})} | custom-call | tf_op jit(solution)/shard_map/pallas_call | solution.py:206
  146.0 20.1 %shard_map.88 = (f32[768,512]{1,0:T(8,128)}, f32[768,64]{1,0:T(8,128)}, f32[192,64,192]{2,1,0:T(8,128)}, bf16[256,1024]{1,0:T(8,128)(2,1)}, bf16[256,1024]{1,0:T...) custom-call(s32[1]{0:T(128)} %bitcast.refs_0_, ...), custom_call_target="tpu_custom_call", output_to_operand_aliasing={{2}: (9, {})} | custom-call | tf_op jit(solution)/shard_map/pallas_call | solution.py:206
  174.1 8.8 %collective-permute-done.3 = bf16[384,576]{1,0:T(8,128)(2,1)S(1)} collective-permute-done((bf16[384,576]{1,0:T(8,128)(2,1)}, bf16[384,576]{1,0:T(8,128)(2,1)S(1)}, u32[]{:S(2)}, u32[]{:S(2)}) %collective-permute-start.3) | collective-permute-done | bytes 442400 | tf_op jit(solution)/shard_map/ppermute | solution.py:19
  185.9 29.4 %collective-permute-done.42 = bf16[256,1024]{1,0:T(8,128)(2,1)S(1)} collective-permute-done((bf16[256,1024]{1,0:T(8,128)(2,1)}, bf16[256,1024]{1,0:T(8,128)(2,1)S(1)}, u32[]{:S(2)}, u32[]{:S(2)}) %collective-permute-start.42) | collective-permute-done | bytes 524320 | tf_op jit(solution)/shard_map/ppermute | solution.py:19
  215.3 1.7 collective-permute-start.38
  217.3 22.7 %collective-permute-done.18 = bf16[256,1024]{1,0:T(8,128)(2,1)S(1)} collective-permute-done((bf16[256,1024]{1,0:T(8,128)(2,1)S(1)}, bf16[256,1024]{1,0:T(8,128)(2,1)S(1)}, u32[]{:S(2)}, u32[]{:S(2)}) %collective-permute-start.18) | collective-permute-done | bytes 524320 | tf_op jit(solution)/shard_map/ppermute | solution.py:19
  240.5 1.8 collective-permute-start.23
  242.5 4.2 collective-permute-done.4
  249.0 4.6 %collective-permute-done.43 = bf16[128,1024]{1,0:T(8,128)(2,1)S(1)} collective-permute-done((bf16[128,1024]{1,0:T(8,128)(2,1)S(1)}, bf16[128,1024]{1,0:T(8,128)(2,1)S(1)}, u32[]{:S(2)}, u32[]{:S(2)}) %collective-permute-start.43) | collective-permute-done | bytes 262176 | tf_op jit(solution)/shard_map/ppermute | solution.py:19
  254.2 1.7 collective-permute-start.30
  256.1 3.9 collective-permute-done.39
  263.8 3.2 collective-permute-done.24
  268.6 3.3 collective-permute-done.44
  273.6 3.3 collective-permute-done.20
  278.6 3.3 collective-permute-done.40
  282.3 1.8 collective-permute-start.34
  284.5 2.7 collective-permute-start.25
  288.8 2.3 collective-permute-start.21
  291.5 13.0 %collective-permute-done.14 = bf16[256,2048]{1,0:T(8,128)(2,1)S(1)} collective-permute-done((bf16[256,2048]{1,0:T(8,128)(2,1)S(1)}, bf16[256,2048]{1,0:T(8,128)(2,1)S(1)}, u32[]{:S(2)}, u32[]{:S(2)}) %collective-permute-start.14) | collective-permute-done | bytes 1048608 | tf_op jit(solution)/shard_map/ppermute | solution.py:19
  306.0 2.8 collective-permute-start.27
  309.3 6.0 %collective-permute-done.7 = bf16[128,2048]{1,0:T(8,128)(2,1)S(1)} collective-permute-done((bf16[128,2048]{1,0:T(8,128)(2,1)S(1)}, bf16[128,2048]{1,0:T(8,128)(2,1)S(1)}, u32[]{:S(2)}, u32[]{:S(2)}) %collective-permute-start.7) | collective-permute-done | bytes 524320 | tf_op jit(solution)/shard_map/ppermute | solution.py:19
  315.3 1.7 collective-permute-start.11
  317.1 2.5 collective-permute-start.31
  319.7 7.7 %collective-permute-done.11 = bf16[128,2048]{1,0:T(8,128)(2,1)S(1)} collective-permute-done((bf16[128,2048]{1,0:T(8,128)(2,1)S(1)}, bf16[128,2048]{1,0:T(8,128)(2,1)S(1)}, u32[]{:S(2)}, u32[]{:S(2)}) %collective-permute-start.11) | collective-permute-done | bytes 524320 | tf_op jit(solution)/shard_map/ppermute | solution.py:19
  327.4 1.7 collective-permute-start.15
  329.2 2.5 collective-permute-start.35
  331.9 5.3 %collective-permute-done.15 = bf16[128,2048]{1,0:T(8,128)(2,1)S(1)} collective-permute-done((bf16[128,2048]{1,0:T(8,128)(2,1)S(1)}, bf16[128,2048]{1,0:T(8,128)(2,1)S(1)}, u32[]{:S(2)}, u32[]{:S(2)}) %collective-permute-start.15) | collective-permute-done | bytes 524320 | tf_op jit(solution)/shard_map/ppermute | solution.py:19
  337.3 2.6 collective-permute-start.41
  340.0 1.6 collective-permute-start.8
  341.8 6.6 %collective-permute-done.8 = bf16[64,2048]{1,0:T(8,128)(2,1)S(1)} collective-permute-done((bf16[64,2048]{1,0:T(8,128)(2,1)S(1)}, bf16[64,2048]{1,0:T(8,128)(2,1)S(1)}, u32[]{:S(2)}, u32[]{:S(2)}) %collective-permute-start.8) | collective-permute-done | bytes 262176 | tf_op jit(solution)/shard_map/ppermute | solution.py:19
  350.1 5.8 %collective-permute-done.28 = bf16[64,2048]{1,0:T(8,128)(2,1)S(1)} collective-permute-done((bf16[64,2048]{1,0:T(8,128)(2,1)S(1)}, bf16[64,2048]{1,0:T(8,128)(2,1)S(1)}, u32[]{:S(2)}, u32[]{:S(2)}) %collective-permute-start.28) | collective-permute-done | bytes 262176 | tf_op jit(solution)/shard_map/ppermute | solution.py:19
  357.5 5.0 %collective-permute-done.12 = bf16[64,2048]{1,0:T(8,128)(2,1)S(1)} collective-permute-done((bf16[64,2048]{1,0:T(8,128)(2,1)S(1)}, bf16[64,2048]{1,0:T(8,128)(2,1)S(1)}, u32[]{:S(2)}, u32[]{:S(2)}) %collective-permute-start.12) | collective-permute-done | bytes 262176 | tf_op jit(solution)/shard_map/ppermute | solution.py:19
  364.2 5.7 %collective-permute-done.32 = bf16[64,2048]{1,0:T(8,128)(2,1)S(1)} collective-permute-done((bf16[64,2048]{1,0:T(8,128)(2,1)S(1)}, bf16[64,2048]{1,0:T(8,128)(2,1)S(1)}, u32[]{:S(2)}, u32[]{:S(2)}) %collective-permute-start.32) | collective-permute-done | bytes 262176 | tf_op jit(solution)/shard_map/ppermute | solution.py:19
  371.5 6.1 %collective-permute-done.16 = bf16[64,2048]{1,0:T(8,128)(2,1)S(1)} collective-permute-done((bf16[64,2048]{1,0:T(8,128)(2,1)S(1)}, bf16[64,2048]{1,0:T(8,128)(2,1)S(1)}, u32[]{:S(2)}, u32[]{:S(2)}) %collective-permute-start.16) | collective-permute-done | bytes 262176 | tf_op jit(solution)/shard_map/ppermute | solution.py:19
  379.3 5.7 %collective-permute-done.36 = bf16[64,2048]{1,0:T(8,128)(2,1)S(1)} collective-permute-done((bf16[64,2048]{1,0:T(8,128)(2,1)S(1)}, bf16[64,2048]{1,0:T(8,128)(2,1)S(1)}, u32[]{:S(2)}, u32[]{:S(2)}) %collective-permute-start.36) | collective-permute-done | bytes 262176 | tf_op jit(solution)/shard_map/ppermute | solution.py:19
  385.0 1.9 collective-permute-start.9
  387.1 5.2 %collective-permute-done.9 = bf16[32,2048]{1,0:T(8,128)(2,1)S(1)} collective-permute-done((bf16[32,2048]{1,0:T(8,128)(2,1)S(1)}, bf16[32,2048]{1,0:T(8,128)(2,1)S(1)}, u32[]{:S(2)}, u32[]{:S(2)}) %collective-permute-start.9) | collective-permute-done | bytes 131104 | tf_op jit(solution)/shard_map/ppermute | solution.py:19
  392.9 8.4 %collective-permute-done.29 = bf16[32,2048]{1,0:T(8,128)(2,1)S(1)} collective-permute-done((bf16[32,2048]{1,0:T(8,128)(2,1)S(1)}, bf16[32,2048]{1,0:T(8,128)(2,1)S(1)}, u32[]{:S(2)}, u32[]{:S(2)}) %collective-permute-start.29) | collective-permute-done | bytes 131104 | tf_op jit(solution)/shard_map/ppermute | solution.py:19
  401.4 8.5 %collective-permute-done.13 = bf16[32,2048]{1,0:T(8,128)(2,1)S(1)} collective-permute-done((bf16[32,2048]{1,0:T(8,128)(2,1)S(1)}, bf16[32,2048]{1,0:T(8,128)(2,1)S(1)}, u32[]{:S(2)}, u32[]{:S(2)}) %collective-permute-start.13) | collective-permute-done | bytes 131104 | tf_op jit(solution)/shard_map/ppermute | solution.py:19
  409.9 6.9 %collective-permute-done.33 = bf16[32,2048]{1,0:T(8,128)(2,1)S(1)} collective-permute-done((bf16[32,2048]{1,0:T(8,128)(2,1)S(1)}, bf16[32,2048]{1,0:T(8,128)(2,1)S(1)}, u32[]{:S(2)}, u32[]{:S(2)}) %collective-permute-start.33) | collective-permute-done | bytes 131104 | tf_op jit(solution)/shard_map/ppermute | solution.py:19
  416.9 6.9 %collective-permute-done.17 = bf16[32,2048]{1,0:T(8,128)(2,1)S(1)} collective-permute-done((bf16[32,2048]{1,0:T(8,128)(2,1)S(1)}, bf16[32,2048]{1,0:T(8,128)(2,1)S(1)}, u32[]{:S(2)}, u32[]{:S(2)}) %collective-permute-start.17) | collective-permute-done | bytes 131104 | tf_op jit(solution)/shard_map/ppermute | solution.py:19
  423.9 5.9 %collective-permute-done.37 = bf16[32,2048]{1,0:T(8,128)(2,1)S(1)} collective-permute-done((bf16[32,2048]{1,0:T(8,128)(2,1)S(1)}, bf16[32,2048]{1,0:T(8,128)(2,1)S(1)}, u32[]{:S(2)}, u32[]{:S(2)}) %collective-permute-start.37) | collective-permute-done | bytes 131104 | tf_op jit(solution)/shard_map/ppermute | solution.py:19
  (165 shorter events, 45.5 us)
Async XLA Ops:
  1.7 11.9 %collective-permute-start.2 = (bf16[192,576]{0,1:T(8,128)(2,1)S(1)}, bf16[192,576]{0,1:T(8,128)(2,1)S(1)}, u32[]{:S(2)}, u32[]{:S(2)}) collective-permute-start(bf16[192,576]{0,1:T(8,128)(2,1)S(1)} %copy.16), channel_id=1, source_target_pairs={{0,6},{2,4},{4,2},{6,0},{8,14},{10,12},{12,10},{14,8},{16,22},{18,... | collective-permute-start | bytes 663560 | tf_op jit(solution)/shard_map/ppermute | solution.py:19
  5.7 13.3 %collective-permute-start.1 = (bf16[192,576]{0,1:T(8,128)(2,1)S(1)}, bf16[192,576]{0,1:T(8,128)(2,1)S(1)}, u32[]{:S(2)}, u32[]{:S(2)}) collective-permute-start(bf16[192,576]{0,1:T(8,128)(2,1)S(1)} %copy.16), channel_id=1, source_target_pairs={{0,4},{2,6},{4,0},{6,2},{8,12},{10,14},{12,8},{14,10},{16,20},{18,... | collective-permute-start | bytes 663560 | tf_op jit(solution)/shard_map/ppermute | solution.py:19
  6.2 13.1 %collective-permute-start = (bf16[192,576]{0,1:T(8,128)(2,1)S(1)}, bf16[192,576]{0,1:T(8,128)(2,1)S(1)}, u32[]{:S(2)}, u32[]{:S(2)}) collective-permute-start(bf16[192,576]{0,1:T(8,128)(2,1)S(1)} %copy.16), channel_id=1, source_target_pairs={{0,2},{2,0},{4,6},{6,4},{8,10},{10,8},{12,14},{14,12},{16,18},{18,... | collective-permute-start | bytes 663560 | tf_op jit(solution)/shard_map/ppermute | solution.py:19
  168.6 14.3 %collective-permute-start.3 = (bf16[384,576]{1,0:T(8,128)(2,1)}, bf16[384,576]{1,0:T(8,128)(2,1)S(1)}, u32[]{:S(2)}, u32[]{:S(2)}) collective-permute-start(bf16[384,576]{1,0:T(8,128)(2,1)} %slice.362), channel_id=1, source_target_pairs={{0,4},{2,6},{4,0},{6,2},{8,12},{10,14},{12,8},{14,10},{16,20},{18,... | collective-permute-start | bytes 1327112 | tf_op jit(solution)/shard_map/ppermute | solution.py:19
  170.0 15.0 %collective-permute-start.22 = (bf16[256,1024]{1,0:T(8,128)(2,1)}, bf16[256,1024]{1,0:T(8,128)(2,1)S(1)}, u32[]{:S(2)}, u32[]{:S(2)}) collective-permute-start(bf16[256,1024]{1,0:T(8,128)(2,1)} %get-tuple-element.63), channel_id=1, source_target_pairs={{0,2},{2,0},{4,6},{6,4},{8,10},{10,8},{12,14},{14,12},{16,18},{18,... | collective-permute-start | bytes 1572872 | tf_op jit(solution)/shard_map/ppermute | solution.py:19
  170.7 111.6 %collective-permute-start.6 = (bf16[256,2048]{1,0:T(8,128)(2,1)}, bf16[256,2048]{1,0:T(8,128)(2,1)S(1)}, u32[]{:S(2)}, u32[]{:S(2)}) collective-permute-start(bf16[256,2048]{1,0:T(8,128)(2,1)} %get-tuple-element.55), channel_id=1, source_target_pairs={{0,2},{2,0},{4,6},{6,4},{8,10},{10,8},{12,14},{14,12},{16,18},{18,... | collective-permute-start | bytes 3145736 | tf_op jit(solution)/shard_map/ppermute | solution.py:19
  172.0 112.5 %collective-permute-start.26 = (bf16[256,2048]{1,0:T(8,128)(2,1)}, bf16[256,2048]{1,0:T(8,128)(2,1)S(1)}, u32[]{:S(2)}, u32[]{:S(2)}) collective-permute-start(bf16[256,2048]{1,0:T(8,128)(2,1)} %get-tuple-element.65), channel_id=1, source_target_pairs={{0,4},{2,6},{4,0},{6,2},{8,12},{10,14},{12,8},{14,10},{16,20},{18,... | collective-permute-start | bytes 3145736 | tf_op jit(solution)/shard_map/ppermute | solution.py:19
  172.6 115.0 %collective-permute-start.10 = (bf16[256,2048]{1,0:T(8,128)(2,1)}, bf16[256,2048]{1,0:T(8,128)(2,1)S(1)}, u32[]{:S(2)}, u32[]{:S(2)}) collective-permute-start(bf16[256,2048]{1,0:T(8,128)(2,1)} %get-tuple-element.57), channel_id=1, source_target_pairs={{0,2},{2,0},{4,6},{6,4},{8,10},{10,8},{12,14},{14,12},{16,18},{18,... | collective-permute-start | bytes 3145736 | tf_op jit(solution)/shard_map/ppermute | solution.py:19
  182.9 34.2 %copy-start.8 = (bf16[256,1024]{1,0:T(8,128)(2,1)S(1)}, bf16[256,1024]{1,0:T(8,128)(2,1)}, u32[]{:S(2)}) copy-start(bf16[256,1024]{1,0:T(8,128)(2,1)} %get-tuple-element.72) | copy-start | bytes 1572868
  182.9 32.5 %collective-permute-start.42 = (bf16[256,1024]{1,0:T(8,128)(2,1)}, bf16[256,1024]{1,0:T(8,128)(2,1)S(1)}, u32[]{:S(2)}, u32[]{:S(2)}) collective-permute-start(bf16[256,1024]{1,0:T(8,128)(2,1)} %get-tuple-element.73), channel_id=1, source_target_pairs={{0,4},{2,6},{4,0},{6,2},{8,12},{10,14},{12,8},{14,10},{16,20},{18,... | collective-permute-start | bytes 1572872 | tf_op jit(solution)/shard_map/ppermute | solution.py:19
  185.0 54.9 %collective-permute-start.18 = (bf16[256,1024]{1,0:T(8,128)(2,1)S(1)}, bf16[256,1024]{1,0:T(8,128)(2,1)S(1)}, u32[]{:S(2)}, u32[]{:S(2)}) collective-permute-start(bf16[256,1024]{1,0:T(8,128)(2,1)S(1)} %copy-done.15), channel_id=1, source_target_pairs={{0,2},{2,0},{4,6},{6,4},{8,10},{10,8},{12,14},{14,12},{16,18},{18,... | collective-permute-start | bytes 1572872 | tf_op jit(solution)/shard_map/ppermute | solution.py:19
  185.7 54.6 %copy-start.7 = (bf16[256,1024]{1,0:T(8,128)(2,1)S(1)}, bf16[256,1024]{1,0:T(8,128)(2,1)}, u32[]{:S(2)}) copy-start(bf16[256,1024]{1,0:T(8,128)(2,1)} %get-tuple-element.60) | copy-start | bytes 1572868
  215.3 25.1 %collective-permute-start.38 = (bf16[256,1024]{1,0:T(8,128)(2,1)S(1)}, bf16[256,1024]{1,0:T(8,128)(2,1)S(1)}, u32[]{:S(2)}, u32[]{:S(2)}) collective-permute-start(bf16[256,1024]{1,0:T(8,128)(2,1)S(1)} %copy-done.14), channel_id=1, source_target_pairs={{0,4},{2,6},{4,0},{6,2},{8,12},{10,14},{12,8},{14,10},{16,20},{18,... | collective-permute-start | bytes 1572872 | tf_op jit(solution)/shard_map/ppermute | solution.py:19
  239.9 6.7 %collective-permute-start.4 = (bf16[192,576]{1,0:T(8,128)(2,1)S(1)}, bf16[192,576]{1,0:T(8,128)(2,1)S(1)}, u32[]{:S(2)}, u32[]{:S(2)}) collective-permute-start(bf16[192,576]{1,0:T(8,128)(2,1)S(1)} %slice.363), channel_id=1, source_target_pairs={{0,2},{2,0},{4,6},{6,4},{8,10},{10,8},{12,14},{14,12},{16,18},{18,... | collective-permute-start | bytes 663560 | tf_op jit(solution)/shard_map/ppermute | solution.py:19
  240.5 6.9 %collective-permute-start.23 = (bf16[128,1024]{1,0:T(8,128)(2,1)S(1)}, bf16[128,1024]{1,0:T(8,128)(2,1)S(1)}, u32[]{:S(2)}, u32[]{:S(2)}) collective-permute-start(bf16[128,1024]{1,0:T(8,128)(2,1)S(1)} %slice.292), channel_id=1, source_target_pairs={{0,4},{2,6},{4,0},{6,2},{8,12},{10,14},{12,8},{14,10},{16,20},{18,... | collective-permute-start | bytes 786440 | tf_op jit(solution)/shard_map/ppermute | solution.py:19
  246.7 6.9 %collective-permute-start.43 = (bf16[128,1024]{1,0:T(8,128)(2,1)S(1)}, bf16[128,1024]{1,0:T(8,128)(2,1)S(1)}, u32[]{:S(2)}, u32[]{:S(2)}) collective-permute-start(bf16[128,1024]{1,0:T(8,128)(2,1)S(1)} %slice.322), channel_id=1, source_target_pairs={{0,2},{2,0},{4,6},{6,4},{8,10},{10,8},{12,14},{14,12},{16,18},{18,... | collective-permute-start | bytes 786440 | tf_op jit(solution)/shard_map/ppermute | solution.py:19
  247.3 6.9 %collective-permute-start.19 = (bf16[128,1024]{1,0:T(8,128)(2,1)S(1)}, bf16[128,1024]{1,0:T(8,128)(2,1)S(1)}, u32[]{:S(2)}, u32[]{:S(2)}) collective-permute-start(bf16[128,1024]{1,0:T(8,128)(2,1)S(1)} %slice.286), channel_id=1, source_target_pairs={{0,4},{2,6},{4,0},{6,2},{8,12},{10,14},{12,8},{14,10},{16,20},{18,... | collective-permute-start | bytes 786440 | tf_op jit(solution)/shard_map/ppermute | solution.py:19
  253.6 6.4 %collective-permute-start.39 = (bf16[128,1024]{1,0:T(8,128)(2,1)S(1)}, bf16[128,1024]{1,0:T(8,128)(2,1)S(1)}, u32[]{:S(2)}, u32[]{:S(2)}) collective-permute-start(bf16[128,1024]{1,0:T(8,128)(2,1)S(1)} %slice.316), channel_id=1, source_target_pairs={{0,2},{2,0},{4,6},{6,4},{8,10},{10,8},{12,14},{14,12},{16,18},{18,... | collective-permute-start | bytes 786440 | tf_op jit(solution)/shard_map/ppermute | solution.py:19
  254.2 34.6 %collective-permute-start.30 = (bf16[256,2048]{1,0:T(8,128)(2,1)S(1)}, bf16[256,2048]{1,0:T(8,128)(2,1)S(1)}, u32[]{:S(2)}, u32[]{:S(2)}) collective-permute-start(bf16[256,2048]{1,0:T(8,128)(2,1)S(1)} %copy-done.13), channel_id=1, source_target_pairs={{0,4},{2,6},{4,0},{6,2},{8,12},{10,14},{12,8},{14,10},{16,20},{18,... | collective-permute-start | bytes 3145736 | tf_op jit(solution)/shard_map/ppermute | solution.py:19
  260.0 1.5 collective-permute-start.5
  261.5 5.5 %collective-permute-start.24 = (bf16[64,1024]{1,0:T(8,128)(2,1)S(1)}, bf16[64,1024]{1,0:T(8,128)(2,1)S(1)}, u32[]{:S(2)}, u32[]{:S(2)}) collective-permute-start(bf16[64,1024]{1,0:T(8,128)(2,1)S(1)} %slice.294), channel_id=1, source_target_pairs={{0,8},{2,10},{4,12},{6,14},{8,0},{10,2},{12,4},{14,6},{16,24},{18,... | collective-permute-start | bytes 393224 | tf_op jit(solution)/shard_map/ppermute | solution.py:19
  267.0 5.0 %collective-permute-start.44 = (bf16[64,1024]{1,0:T(8,128)(2,1)S(1)}, bf16[64,1024]{1,0:T(8,128)(2,1)S(1)}, u32[]{:S(2)}, u32[]{:S(2)}) collective-permute-start(bf16[64,1024]{1,0:T(8,128)(2,1)S(1)} %slice.324), channel_id=1, source_target_pairs={{0,8},{2,10},{4,12},{6,14},{8,0},{10,2},{12,4},{14,6},{16,24},{18,... | collective-permute-start | bytes 393224 | tf_op jit(solution)/shard_map/ppermute | solution.py:19
  272.0 5.0 %collective-permute-start.20 = (bf16[64,1024]{1,0:T(8,128)(2,1)S(1)}, bf16[64,1024]{1,0:T(8,128)(2,1)S(1)}, u32[]{:S(2)}, u32[]{:S(2)}) collective-permute-start(bf16[64,1024]{1,0:T(8,128)(2,1)S(1)} %slice.288), channel_id=1, source_target_pairs={{0,8},{2,10},{4,12},{6,14},{8,0},{10,2},{12,4},{14,6},{16,24},{18,... | collective-permute-start | bytes 393224 | tf_op jit(solution)/shard_map/ppermute | solution.py:19
  276.9 5.0 %collective-permute-start.40 = (bf16[64,1024]{1,0:T(8,128)(2,1)S(1)}, bf16[64,1024]{1,0:T(8,128)(2,1)S(1)}, u32[]{:S(2)}, u32[]{:S(2)}) collective-permute-start(bf16[64,1024]{1,0:T(8,128)(2,1)S(1)} %slice.318), channel_id=1, source_target_pairs={{0,8},{2,10},{4,12},{6,14},{8,0},{10,2},{12,4},{14,6},{16,24},{18,... | collective-permute-start | bytes 393224 | tf_op jit(solution)/shard_map/ppermute | solution.py:19
  281.9 22.6 %collective-permute-start.14 = (bf16[256,2048]{1,0:T(8,128)(2,1)S(1)}, bf16[256,2048]{1,0:T(8,128)(2,1)S(1)}, u32[]{:S(2)}, u32[]{:S(2)}) collective-permute-start(bf16[256,2048]{1,0:T(8,128)(2,1)S(1)} %copy-done.12), channel_id=1, source_target_pairs={{0,2},{2,0},{4,6},{6,4},{8,10},{10,8},{12,14},{14,12},{16,18},{18,... | collective-permute-start | bytes 3145736 | tf_op jit(solution)/shard_map/ppermute | solution.py:19
  282.3 23.7 %collective-permute-start.34 = (bf16[256,2048]{1,0:T(8,128)(2,1)S(1)}, bf16[256,2048]{1,0:T(8,128)(2,1)S(1)}, u32[]{:S(2)}, u32[]{:S(2)}) collective-permute-start(bf16[256,2048]{1,0:T(8,128)(2,1)S(1)} %copy-done.11), channel_id=1, source_target_pairs={{0,4},{2,6},{4,0},{6,2},{8,12},{10,14},{12,8},{14,10},{16,20},{18,... | collective-permute-start | bytes 3145736 | tf_op jit(solution)/shard_map/ppermute | solution.py:19
  284.5 145.3 %collective-permute-start.25 = (bf16[32,1024]{1,0:T(8,128)(2,1)S(1)}, bf16[32,1024]{1,0:T(8,128)(2,1)S(1)}, u32[]{:S(2)}, u32[]{:S(2)}) collective-permute-start(bf16[32,1024]{1,0:T(8,128)(2,1)S(1)} %slice.296), channel_id=1, source_target_pairs={{0,16},{2,18},{4,20},{6,22},{8,24},{10,26},{12,28},{14,30},{16,0},... | collective-permute-start | bytes 196616 | tf_op jit(solution)/shard_map/ppermute | solution.py:19
  287.7 143.4 %collective-permute-start.45 = (bf16[32,1024]{1,0:T(8,128)(2,1)S(1)}, bf16[32,1024]{1,0:T(8,128)(2,1)S(1)}, u32[]{:S(2)}, u32[]{:S(2)}) collective-permute-start(bf16[32,1024]{1,0:T(8,128)(2,1)S(1)} %slice.326), channel_id=1, source_target_pairs={{0,16},{2,18},{4,20},{6,22},{8,24},{10,26},{12,28},{14,30},{16,0},... | collective-permute-start | bytes 196616 | tf_op jit(solution)/shard_map/ppermute | solution.py:19
  288.8 141.0 %collective-permute-start.21 = (bf16[32,1024]{1,0:T(8,128)(2,1)S(1)}, bf16[32,1024]{1,0:T(8,128)(2,1)S(1)}, u32[]{:S(2)}, u32[]{:S(2)}) collective-permute-start(bf16[32,1024]{1,0:T(8,128)(2,1)S(1)} %slice.290), channel_id=1, source_target_pairs={{0,16},{2,18},{4,20},{6,22},{8,24},{10,26},{12,28},{14,30},{16,0},... | collective-permute-start | bytes 196616 | tf_op jit(solution)/shard_map/ppermute | solution.py:19
  304.5 10.8 %collective-permute-start.7 = (bf16[128,2048]{1,0:T(8,128)(2,1)S(1)}, bf16[128,2048]{1,0:T(8,128)(2,1)S(1)}, u32[]{:S(2)}, u32[]{:S(2)}) collective-permute-start(bf16[128,2048]{1,0:T(8,128)(2,1)S(1)} %slice.268), channel_id=1, source_target_pairs={{0,4},{2,6},{4,0},{6,2},{8,12},{10,14},{12,8},{14,10},{16,20},{18,... | collective-permute-start | bytes 1572872 | tf_op jit(solution)/shard_map/ppermute | solution.py:19
  306.0 11.1 %collective-permute-start.27 = (bf16[128,2048]{1,0:T(8,128)(2,1)S(1)}, bf16[128,2048]{1,0:T(8,128)(2,1)S(1)}, u32[]{:S(2)}, u32[]{:S(2)}) collective-permute-start(bf16[128,2048]{1,0:T(8,128)(2,1)S(1)} %slice.298), channel_id=1, source_target_pairs={{0,2},{2,0},{4,6},{6,4},{8,10},{10,8},{12,14},{14,12},{16,18},{18,... | collective-permute-start | bytes 1572872 | tf_op jit(solution)/shard_map/ppermute | solution.py:19
  315.3 12.1 %collective-permute-start.11 = (bf16[128,2048]{1,0:T(8,128)(2,1)S(1)}, bf16[128,2048]{1,0:T(8,128)(2,1)S(1)}, u32[]{:S(2)}, u32[]{:S(2)}) collective-permute-start(bf16[128,2048]{1,0:T(8,128)(2,1)S(1)} %slice.274), channel_id=1, source_target_pairs={{0,4},{2,6},{4,0},{6,2},{8,12},{10,14},{12,8},{14,10},{16,20},{18,... | collective-permute-start | bytes 1572872 | tf_op jit(solution)/shard_map/ppermute | solution.py:19
  317.1 12.1 %collective-permute-start.31 = (bf16[128,2048]{1,0:T(8,128)(2,1)S(1)}, bf16[128,2048]{1,0:T(8,128)(2,1)S(1)}, u32[]{:S(2)}, u32[]{:S(2)}) collective-permute-start(bf16[128,2048]{1,0:T(8,128)(2,1)S(1)} %slice.304), channel_id=1, source_target_pairs={{0,2},{2,0},{4,6},{6,4},{8,10},{10,8},{12,14},{14,12},{16,18},{18,... | collective-permute-start | bytes 1572872 | tf_op jit(solution)/shard_map/ppermute | solution.py:19
  327.4 9.9 %collective-permute-start.15 = (bf16[128,2048]{1,0:T(8,128)(2,1)S(1)}, bf16[128,2048]{1,0:T(8,128)(2,1)S(1)}, u32[]{:S(2)}, u32[]{:S(2)}) collective-permute-start(bf16[128,2048]{1,0:T(8,128)(2,1)S(1)} %slice.280), channel_id=1, source_target_pairs={{0,4},{2,6},{4,0},{6,2},{8,12},{10,14},{12,8},{14,10},{16,20},{18,... | collective-permute-start | bytes 1572872 | tf_op jit(solution)/shard_map/ppermute | solution.py:19
  329.2 10.8 %collective-permute-start.35 = (bf16[128,2048]{1,0:T(8,128)(2,1)S(1)}, bf16[128,2048]{1,0:T(8,128)(2,1)S(1)}, u32[]{:S(2)}, u32[]{:S(2)}) collective-permute-start(bf16[128,2048]{1,0:T(8,128)(2,1)S(1)} %slice.310), channel_id=1, source_target_pairs={{0,2},{2,0},{4,6},{6,4},{8,10},{10,8},{12,14},{14,12},{16,18},{18,... | collective-permute-start | bytes 1572872 | tf_op jit(solution)/shard_map/ppermute | solution.py:19
  337.3 92.6 %collective-permute-start.41 = (bf16[32,1024]{1,0:T(8,128)(2,1)S(1)}, bf16[32,1024]{1,0:T(8,128)(2,1)S(1)}, u32[]{:S(2)}, u32[]{:S(2)}) collective-permute-start(bf16[32,1024]{1,0:T(8,128)(2,1)S(1)} %slice.320), channel_id=1, source_target_pairs={{0,16},{2,18},{4,20},{6,22},{8,24},{10,26},{12,28},{14,30},{16,0},... | collective-permute-start | bytes 196616 | tf_op jit(solution)/shard_map/ppermute | solution.py:19
  340.0 8.4 %collective-permute-start.8 = (bf16[64,2048]{1,0:T(8,128)(2,1)S(1)}, bf16[64,2048]{1,0:T(8,128)(2,1)S(1)}, u32[]{:S(2)}, u32[]{:S(2)}) collective-permute-start(bf16[64,2048]{1,0:T(8,128)(2,1)S(1)} %slice.270), channel_id=1, source_target_pairs={{0,8},{2,10},{4,12},{6,14},{8,0},{10,2},{12,4},{14,6},{16,24},{18,... | collective-permute-start | bytes 786440 | tf_op jit(solution)/shard_map/ppermute | solution.py:19
  348.4 7.5 %collective-permute-start.28 = (bf16[64,2048]{1,0:T(8,128)(2,1)S(1)}, bf16[64,2048]{1,0:T(8,128)(2,1)S(1)}, u32[]{:S(2)}, u32[]{:S(2)}) collective-permute-start(bf16[64,2048]{1,0:T(8,128)(2,1)S(1)} %slice.300), channel_id=1, source_target_pairs={{0,8},{2,10},{4,12},{6,14},{8,0},{10,2},{12,4},{14,6},{16,24},{18,... | collective-permute-start | bytes 786440 | tf_op jit(solution)/shard_map/ppermute | solution.py:19
  355.9 6.6 %collective-permute-start.12 = (bf16[64,2048]{1,0:T(8,128)(2,1)S(1)}, bf16[64,2048]{1,0:T(8,128)(2,1)S(1)}, u32[]{:S(2)}, u32[]{:S(2)}) collective-permute-start(bf16[64,2048]{1,0:T(8,128)(2,1)S(1)} %slice.276), channel_id=1, source_target_pairs={{0,8},{2,10},{4,12},{6,14},{8,0},{10,2},{12,4},{14,6},{16,24},{18,... | collective-permute-start | bytes 786440 | tf_op jit(solution)/shard_map/ppermute | solution.py:19
  362.5 7.4 %collective-permute-start.32 = (bf16[64,2048]{1,0:T(8,128)(2,1)S(1)}, bf16[64,2048]{1,0:T(8,128)(2,1)S(1)}, u32[]{:S(2)}, u32[]{:S(2)}) collective-permute-start(bf16[64,2048]{1,0:T(8,128)(2,1)S(1)} %slice.306), channel_id=1, source_target_pairs={{0,8},{2,10},{4,12},{6,14},{8,0},{10,2},{12,4},{14,6},{16,24},{18,... | collective-permute-start | bytes 786440 | tf_op jit(solution)/shard_map/ppermute | solution.py:19
  369.9 7.8 %collective-permute-start.16 = (bf16[64,2048]{1,0:T(8,128)(2,1)S(1)}, bf16[64,2048]{1,0:T(8,128)(2,1)S(1)}, u32[]{:S(2)}, u32[]{:S(2)}) collective-permute-start(bf16[64,2048]{1,0:T(8,128)(2,1)S(1)} %slice.282), channel_id=1, source_target_pairs={{0,8},{2,10},{4,12},{6,14},{8,0},{10,2},{12,4},{14,6},{16,24},{18,... | collective-permute-start | bytes 786440 | tf_op jit(solution)/shard_map/ppermute | solution.py:19
  377.7 7.3 %collective-permute-start.36 = (bf16[64,2048]{1,0:T(8,128)(2,1)S(1)}, bf16[64,2048]{1,0:T(8,128)(2,1)S(1)}, u32[]{:S(2)}, u32[]{:S(2)}) collective-permute-start(bf16[64,2048]{1,0:T(8,128)(2,1)S(1)} %slice.312), channel_id=1, source_target_pairs={{0,8},{2,10},{4,12},{6,14},{8,0},{10,2},{12,4},{14,6},{16,24},{18,... | collective-permute-start | bytes 786440 | tf_op jit(solution)/shard_map/ppermute | solution.py:19
  385.0 7.3 %collective-permute-start.9 = (bf16[32,2048]{1,0:T(8,128)(2,1)S(1)}, bf16[32,2048]{1,0:T(8,128)(2,1)S(1)}, u32[]{:S(2)}, u32[]{:S(2)}) collective-permute-start(bf16[32,2048]{1,0:T(8,128)(2,1)S(1)} %slice.272), channel_id=1, source_target_pairs={{0,16},{2,18},{4,20},{6,22},{8,24},{10,26},{12,28},{14,30},{16,0},... | collective-permute-start | bytes 393224 | tf_op jit(solution)/shard_map/ppermute | solution.py:19
  392.3 9.1 %collective-permute-start.29 = (bf16[32,2048]{1,0:T(8,128)(2,1)S(1)}, bf16[32,2048]{1,0:T(8,128)(2,1)S(1)}, u32[]{:S(2)}, u32[]{:S(2)}) collective-permute-start(bf16[32,2048]{1,0:T(8,128)(2,1)S(1)} %slice.302), channel_id=1, source_target_pairs={{0,16},{2,18},{4,20},{6,22},{8,24},{10,26},{12,28},{14,30},{16,0},... | collective-permute-start | bytes 393224 | tf_op jit(solution)/shard_map/ppermute | solution.py:19
  401.4 8.5 %collective-permute-start.13 = (bf16[32,2048]{1,0:T(8,128)(2,1)S(1)}, bf16[32,2048]{1,0:T(8,128)(2,1)S(1)}, u32[]{:S(2)}, u32[]{:S(2)}) collective-permute-start(bf16[32,2048]{1,0:T(8,128)(2,1)S(1)} %slice.278), channel_id=1, source_target_pairs={{0,16},{2,18},{4,20},{6,22},{8,24},{10,26},{12,28},{14,30},{16,0},... | collective-permute-start | bytes 393224 | tf_op jit(solution)/shard_map/ppermute | solution.py:19
  409.9 7.0 %collective-permute-start.33 = (bf16[32,2048]{1,0:T(8,128)(2,1)S(1)}, bf16[32,2048]{1,0:T(8,128)(2,1)S(1)}, u32[]{:S(2)}, u32[]{:S(2)}) collective-permute-start(bf16[32,2048]{1,0:T(8,128)(2,1)S(1)} %slice.308), channel_id=1, source_target_pairs={{0,16},{2,18},{4,20},{6,22},{8,24},{10,26},{12,28},{14,30},{16,0},... | collective-permute-start | bytes 393224 | tf_op jit(solution)/shard_map/ppermute | solution.py:19
  416.9 7.0 %collective-permute-start.17 = (bf16[32,2048]{1,0:T(8,128)(2,1)S(1)}, bf16[32,2048]{1,0:T(8,128)(2,1)S(1)}, u32[]{:S(2)}, u32[]{:S(2)}) collective-permute-start(bf16[32,2048]{1,0:T(8,128)(2,1)S(1)} %slice.284), channel_id=1, source_target_pairs={{0,16},{2,18},{4,20},{6,22},{8,24},{10,26},{12,28},{14,30},{16,0},... | collective-permute-start | bytes 393224 | tf_op jit(solution)/shard_map/ppermute | solution.py:19
  423.8 6.0 %collective-permute-start.37 = (bf16[32,2048]{1,0:T(8,128)(2,1)S(1)}, bf16[32,2048]{1,0:T(8,128)(2,1)S(1)}, u32[]{:S(2)}, u32[]{:S(2)}) collective-permute-start(bf16[32,2048]{1,0:T(8,128)(2,1)S(1)} %slice.314), channel_id=1, source_target_pairs={{0,16},{2,18},{4,20},{6,22},{8,24},{10,26},{12,28},{14,30},{16,0},... | collective-permute-start | bytes 393224 | tf_op jit(solution)/shard_map/ppermute | solution.py:19
  (14 other events, 226.2 us)
